TPU v7x, 32 devices: a whole 2x2x4 slice. The times are simulated.
32 devices in a mesh: tenant: 2 (over y), ctx: 2 (over x), head: 8 (over z, core).
Axes of the slice: x: 2, y: 2, z: 4, core: 2. Of those that a mesh axis runs over, the one named last changes fastest.
Arguments:
- tokens: bfloat16 [1024, 4608], P(('tenant', 'ctx'), 'head'), parts along dimension 0, may hold values from -6 to 6
- query_frozen_matrix: bfloat16 [4608, 2048], P('ctx', 'head'), may hold values from -0.09375 to 0.09375
- key_weight: bfloat16 [4608, 1024], P('ctx', 'head'), may hold values from -0.09375 to 0.09375
- value_frozen_matrix: bfloat16 [4608, 1024], P('ctx', 'head'), may hold values from -0.09375 to 0.09375
- query_down: bfloat16 [9216, 16], P('tenant'), parts along dimension 0, may hold values from -0.09375 to 0.09375
- query_adapter_expand: bfloat16 [32, 2048], P('tenant', 'head'), parts along dimension 0, may hold values from -1.5 to 1.5
- value_down: bfloat16 [9216, 16], P('tenant'), parts along dimension 0, may hold values from -0.09375 to 0.09375
- value_adapter_expand: bfloat16 [32, 1024], P('tenant', 'head'), parts along dimension 0, may hold values from -1.5 to 1.5
- block_order: int32 [8], P('tenant'), parts along dimension 0, may hold values from 0 to 3, each once
- doc_starts: int32 [24], P('tenant'), parts along dimension 0, may hold values from 0 to 511, as said below
- prompt_of: int32 [24], P('tenant'), parts along dimension 0, may hold values from 0 to 11, as said below
Outputs:
- attended: bfloat16 [1024, 2048], P(('tenant', 'ctx'), 'head'), parts along dimension 0
There are 2 independent parts, one for each index of `tenant`. A program takes and returns all parts, laid end to end along the dimension named above; an argument that names none is the same for every part. Nothing has to cross between parts.
Inputs may be any that keep to these rules, and one draw needn't show every extreme that they name: `doc_starts`: strictly increasing with first entry 0; the segments come in 4 groups of three: a prompt, a chosen and a rejected response. `prompt_of`: for segment j = 3k it is j; for j = 3k + 1 it is 3k; for j = 3k + 2 it is 3k or j. `block_order`: each of 0 to 3 once.
All inputs are finite; a program needn't handle non-finite values.
Results may differ from a plain program's by a relative error of at most 0.012.
Values may be sent and summed in bfloat16 or wider, within the bound.
No kernel may reach another device: no remote copies, remote signals or barrier semaphores. Data moves between devices by JAX's collectives and lax.ppermute only.
A program may use at most 64 MiB of HBM per device.

v0:
```python
import math

import jax
import jax.numpy as jnp
from jax import lax
from jax.sharding import PartitionSpec as P

HD = 128


softcap_limit = 50.0
query_scale = 144.0 ** (-0.5)
adapter_scaling = 2.0
rope_base = 10000.0


def row_meta(row_ids, block_order, doc_starts, prompt_of, block_len, sequence_len):
    block_count = block_order.shape[0]
    block_id = row_ids // block_len
    one_hot = block_id[:, None] == jnp.arange(block_count, dtype=jnp.int32)[None, :]
    ordered = jnp.sum(jnp.where(one_hot, block_order[None, :], 0), axis=1)
    places = ordered * block_len + row_ids % block_len
    segment = jnp.sum((doc_starts[None, :] <= places[:, None]).astype(jnp.int32), axis=1) - 1
    seg_ids = jnp.arange(doc_starts.shape[0], dtype=jnp.int32)
    selected = segment[:, None] == seg_ids[None, :]
    prompt_seg = jnp.sum(jnp.where(selected, prompt_of[None, :], 0), axis=1)
    own_start = jnp.sum(jnp.where(selected, doc_starts[None, :], 0), axis=1)
    next_starts = jnp.concatenate([doc_starts[1:], jnp.full((1,), sequence_len, jnp.int32)])
    prompt_sel = prompt_seg[:, None] == seg_ids[None, :]
    prompt_len = jnp.sum(jnp.where(prompt_sel, (next_starts - doc_starts)[None, :], 0), axis=1)
    rotary_pos = places - own_start + jnp.where(prompt_seg != segment, prompt_len, 0)
    return (places, segment, prompt_seg, rotary_pos)


def rotate(values_in, rotary_pos):
    width_half = values_in.shape[-1] // 2
    frequency = jnp.exp(
        jnp.arange(width_half, dtype=jnp.float32)
        * (-2.0 * math.log(rope_base) / values_in.shape[-1])
    )
    angles = rotary_pos.astype(jnp.float32)[:, None] * frequency[None, :]
    cosine = jnp.concatenate([jnp.cos(angles), jnp.cos(angles)], axis=-1)[:, None, :]
    sine_part = jnp.concatenate([jnp.sin(angles), jnp.sin(angles)], axis=-1)[:, None, :]
    rotated = jnp.concatenate([-values_in[..., width_half:], values_in[..., :width_half]], axis=-1)
    return values_in * cosine + rotated * sine_part


def visible_mask(query_info, key_info):
    same_doc = (key_info[1][None, :] == query_info[1][:, None]) & (
        key_info[0][None, :] <= query_info[0][:, None]
    )
    from_prompt = (key_info[1][None, :] == query_info[2][:, None]) & (
        query_info[2] != query_info[1]
    )[:, None]
    return same_doc | from_prompt


def local(
    tokens,
    query_frozen_matrix,
    key_weight,
    value_frozen_matrix,
    query_down,
    query_adapter_expand,
    value_down,
    value_adapter_expand,
    block_order,
    doc_starts,
    prompt_of,
):
    tok_rows = tokens.shape[0]
    cycle_size = lax.axis_size("ctx")
    device = lax.axis_index("ctx")
    sequence_len = tok_rows * cycle_size
    block_len = tok_rows // 2
    full_tokens = lax.all_gather(tokens, "head", axis=1, tiled=True)

    def add_rows(weight_part):
        return jnp.dot(full_tokens, weight_part, preferred_element_type=jnp.float32)

    frozen_query_output = add_rows(lax.all_gather(query_frozen_matrix, "ctx", axis=0, tiled=True))
    key_base = add_rows(lax.all_gather(key_weight, "ctx", axis=0, tiled=True))
    frozen_value_output = add_rows(lax.all_gather(value_frozen_matrix, "ctx", axis=0, tiled=True))
    own_ids = device * tok_rows + jnp.arange(tok_rows, dtype=jnp.int32)
    own_info = row_meta(own_ids, block_order, doc_starts, prompt_of, block_len, sequence_len)
    local_heads = query_frozen_matrix.shape[1] // HD
    local_kv = key_weight.shape[1] // HD
    per_kv = local_heads // local_kv
    query_adapter_hidden = jnp.dot(
        full_tokens, query_down, preferred_element_type=jnp.float32
    ).astype(jnp.bfloat16)
    query_states = frozen_query_output + adapter_scaling * jnp.dot(
        query_adapter_hidden, query_adapter_expand, preferred_element_type=jnp.float32
    )
    query_states = (
        rotate(query_states.reshape(tok_rows, local_heads, HD), own_info[3]) * query_scale
    ).astype(jnp.bfloat16)
    query_heads = query_states.reshape(tok_rows, local_kv, per_kv, HD)
    key_proj = (
        rotate(key_base.reshape(tok_rows, local_kv, HD), own_info[3])
        .astype(jnp.bfloat16)
        .reshape(tok_rows, local_kv * HD)
    )
    value_adapter_hidden = jnp.dot(
        full_tokens, value_down, preferred_element_type=jnp.float32
    ).astype(jnp.bfloat16)
    value_projected = (
        frozen_value_output
        + adapter_scaling
        * jnp.dot(value_adapter_hidden, value_adapter_expand, preferred_element_type=jnp.float32)
    ).astype(jnp.bfloat16)
    pieces = (
        lax.all_gather(key_proj, "ctx", axis=0, tiled=True),
        lax.all_gather(value_projected, "ctx", axis=0, tiled=True),
    )
    key_ids = jnp.arange(pieces[0].shape[0], dtype=jnp.int32)
    key_block = pieces[0]
    value_block = pieces[1]
    key_info = row_meta(key_ids, block_order, doc_starts, prompt_of, block_len, sequence_len)
    visible = visible_mask(own_info, key_info)
    key_heads = key_block.reshape(key_block.shape[0], local_kv, HD)
    value_heads = value_block.reshape(value_block.shape[0], local_kv, HD)
    scores = jnp.einsum(
        "tkgd,skd->kgts", query_heads, key_heads, preferred_element_type=jnp.float32
    )
    capped = softcap_limit * jnp.tanh(scores / softcap_limit)
    unnorm = jnp.where(visible[None, None], jnp.exp(capped), jnp.zeros_like(capped))
    denominator = jnp.sum(unnorm, axis=-1)
    numerator = jnp.einsum(
        "kgts,skd->tkgd",
        unnorm.astype(jnp.bfloat16),
        value_heads,
        preferred_element_type=jnp.float32,
    )
    numerator, denominator = (numerator, denominator)
    attended = numerator / jnp.transpose(denominator, (2, 0, 1))[..., None]
    return attended.reshape(tok_rows, local_heads * HD).astype(jnp.bfloat16)


def solution(mesh):
    in_specs = (
        P(("tenant", "ctx"), "head"),
        P("ctx", "head"),
        P("ctx", "head"),
        P("ctx", "head"),
        P("tenant", None),
        P("tenant", "head"),
        P("tenant", None),
        P("tenant", "head"),
        P("tenant"),
        P("tenant"),
        P("tenant"),
    )
    out_specs = P(("tenant", "ctx"), "head")
    return jax.shard_map(local, mesh=mesh, in_specs=in_specs, out_specs=out_specs, check_vma=False)
```

profile of v0, /device:TPU:16, one launch (start us, length us, event | category | flops | bytes accessed | tf_op | source)
XLA Modules:
  0.0 141.9 jit_solution(536576771758366168)
XLA Ops:
  6.5 0.0 all-gather.9.cloned.1.call-start
  6.6 0.7 all-gather.9.cloned.1.call-update
  7.3 0.0 all-gather.5.cloned.1.call-start
  7.3 0.7 all-gather.5.cloned.1.call-update
  8.0 0.0 all-gather.11.cloned.1.call-start
  8.1 0.7 all-gather.11.cloned.1.call-update
  8.8 0.0 all-gather.7.cloned.1.call-start
  8.8 0.5 all-gather.7.cloned.1.call-update
  9.4 0.1 slice.15
  9.5 0.1 select_reduce_fusion.4
  9.6 0.1 convert_reduce_fusion.1
  9.7 0.1 select_reduce_fusion.3
  9.7 0.1 convert_reduce_fusion
  9.8 0.1 add_subtract_fusion
  9.9 0.1 select_reduce_fusion.1
  10.0 0.1 select_reduce_fusion
  10.1 0.3 multiply_cosine_fusion
  10.4 0.2 and_or_fusion
  10.7 22.1 %all-gather.9.cloned.1.call-done = bf16[4608,128]{1,0:T(8,128)(2,1)} async-done(((bf16[2304,128]{1,0:T(8,128)(2,1)}), bf16[4608,128]{1,0:T(8,128)(2,1)}) %all-gather.9.cloned.1.call-update) | async-done | bytes 1179664 | tf_op jit(solution)/shard_map/all_gather | solution.py:82
  32.8 32.4 %all-gather.5.cloned.1.call-done = bf16[256,4608]{0,1:T(8,128)(2,1)} async-done(((bf16[256,576]{0,1:T(8,128)(2,1)}), bf16[256,4608]{0,1:T(8,128)(2,1)}) %all-gather.5.cloned.1.call-update) | async-done | bytes 2359312 | tf_op jit(solution)/shard_map/all_gather | solution.py:76
  65.1 2.7 %fusion.30 = f32[256,128]{0,1:T(8,128)S(1)} fusion(bf16[256,4608]{0,1:T(8,128)(2,1)} %all-gather.5.cloned.1.call-done, bf16[4608,128]{1,0:T(8,128)(2,1)} %all-gather.9.cloned.1.call-done), kind=kOutput, calls=%fused_computation.76 | convolution fusion | flops 301989888 | bytes 3670016 | tf_op jit(solution)/shard_map/dot_general | solution.py:79
  67.9 4.9 %all_gather.22 = bf16[512,128]{0,1:T(8,128)(2,1)S(1)} all-gather(bf16[256,128]{0,1:T(8,128)(2,1)S(1)} %get-tuple-element.13), channel_id=1, replica_groups=mesh['tenant'=2,'ctx'=2,'head'=8] {'ctx'}, dimensions={0}, use_global_device_ids=true | all-gather | bytes 196608 | tf_op jit(solution)/shard_map/all_gather | solution.py:113
  72.9 1.0 convolution_multiply_fusion.1
  73.9 28.9 %all-gather.11.cloned.1.call-done = bf16[4608,256]{1,0:T(8,128)(2,1)} async-done(((bf16[2304,256]{1,0:T(8,128)(2,1)}), bf16[4608,256]{1,0:T(8,128)(2,1)}) %all-gather.11.cloned.1.call-update) | async-done | bytes 2359312 | tf_op jit(solution)/shard_map/all_gather | solution.py:81
  102.8 2.7 %convolution_add_fusion = f32[256,256]{0,1:T(8,128)S(1)} fusion(f32[256,256]{0,1:T(8,128)S(1)} %convolution_multiply_fusion.1, bf16[256,4608]{0,1:T(8,128)(2,1)S(1)} %copy-done.4, bf16[4608,256]{1,0:T(8,128)(2,1)} %all-gather.11.cloned.1.call-done), kind=kOutput, calls=%fused_computation.7 | convolution fusion | flops 604045312 | bytes 5242880 | tf_op jit(solution)/shard_map/dot_general | solution.py:79
  105.5 2.5 %convolution_multiply_fusion.2 = f32[256,128]{0,1:T(8,128)} fusion(bf16[16,128]{1,0:T(8,128)(2,1)} %param.18, bf16[256,4608]{0,1:T(8,128)(2,1)S(1)} %copy-done.4, bf16[4608,16]{0,1:T(8,128)(2,1)} %param.17), kind=kOutput, calls=%fused_computation.10 | convolution fusion | flops 38834176 | bytes 2641920 | tf_op jit(solution)/shard_map/dot_general | solution.py:110
  108.0 18.9 %all-gather.7.cloned.1.call-done = bf16[4608,128]{1,0:T(8,128)(2,1)} async-done(((bf16[2304,128]{1,0:T(8,128)(2,1)}), bf16[4608,128]{1,0:T(8,128)(2,1)}) %all-gather.7.cloned.1.call-update) | async-done | bytes 1179664 | tf_op jit(solution)/shard_map/all_gather | solution.py:83
  126.9 1.9 %fusion.5 = bf16[256,128]{0,1:T(8,128)(2,1)S(1)} fusion(f32[256,128]{0,1:T(8,128)} %convolution_multiply_fusion.2, bf16[256,4608]{0,1:T(8,128)(2,1)S(1)} %copy-done.4, bf16[4608,128]{1,0:T(8,128)(2,1)} %all-gather.7.cloned.1.call-done), kind=kOutput, calls=%fused_computation.11 | convolution fusion | flops 302055424 | bytes 3735552 | tf_op jit(solution)/shard_map/dot_general | solution.py:79
  128.8 4.9 %all_gather.20 = bf16[512,128]{0,1:T(8,128)(2,1)S(1)} all-gather(bf16[256,128]{0,1:T(8,128)(2,1)S(1)} %fusion.5), channel_id=1, replica_groups=mesh['tenant'=2,'ctx'=2,'head'=8] {'ctx'}, dimensions={0}, use_global_device_ids=true | all-gather | bytes 196608 | tf_op jit(solution)/shard_map/all_gather | solution.py:114
  133.9 0.5 fusion.29
  134.4 0.2 fusion.7
  134.6 0.8 copy.19
  (25 shorter events, 0.2 us)
Async XLA Ops:
  6.5 66.3 %copy-start = (bf16[4608,16]{0,1:T(8,128)(2,1)S(1)}, bf16[4608,16]{0,1:T(8,128)(2,1)}, u32[]{:S(2)}) copy-start(bf16[4608,16]{0,1:T(8,128)(2,1)} %param.15) | copy-start | bytes 442372
  6.5 2.8 %copy-start.1 = (s32[12]{0:T(128)S(1)}, s32[12]{0:T(128)}, u32[]{:S(2)}) copy-start(s32[12]{0:T(128)} %param.20) | copy-start | bytes 148
  6.5 2.9 %copy-start.2 = (s32[4]{0:T(128)S(1)}, s32[4]{0:T(128)}, u32[]{:S(2)}) copy-start(s32[4]{0:T(128)} %param.19) | copy-start | bytes 52
  6.5 3.4 %copy-start.3 = (s32[12]{0:T(128)S(1)}, s32[12]{0:T(128)}, u32[]{:S(2)}) copy-start(s32[12]{0:T(128)} %param.21) | copy-start | bytes 148
  6.5 26.2 %all-gather.9.cloned.1.call-start = ((), (), s32[]{:S(2)}) async-start(), calls=%async_computation.2 | async-start | bytes 1769472 | tf_op jit(solution)/shard_map/all_gather | solution.py:82
  7.3 57.9 %all-gather.5.cloned.1.call-start = ((), (), s32[]{:S(2)}) async-start(), calls=%async_computation | async-start | bytes 2654208 | tf_op jit(solution)/shard_map/all_gather | solution.py:76
  8.0 94.7 %all-gather.11.cloned.1.call-start = ((), (), s32[]{:S(2)}) async-start(), calls=%async_computation.3 | async-start | bytes 3538944 | tf_op jit(solution)/shard_map/all_gather | solution.py:81
  8.8 118.2 %all-gather.7.cloned.1.call-start = ((), (), s32[]{:S(2)}) async-start(), calls=%async_computation.1 | async-start | bytes 1769472 | tf_op jit(solution)/shard_map/all_gather | solution.py:83
  10.7 62.2 %copy-start.5 = (bf16[16,256]{1,0:T(8,128)(2,1)S(1)}, bf16[16,256]{1,0:T(8,128)(2,1)}, u32[]{:S(2)}) copy-start(bf16[16,256]{1,0:T(8,128)(2,1)} %param.16) | copy-start | bytes 24580
  65.1 7.8 %copy-start.4 = (bf16[256,4608]{0,1:T(8,128)(2,1)S(1)}, bf16[256,4608]{0,1:T(8,128)(2,1)}, u32[]{:S(2)}) copy-start(bf16[256,4608]{0,1:T(8,128)(2,1)} %all-gather.5.cloned.1.call-done) | copy-start | bytes 7077892
Sparse Core Ops, SparseCore 0:
  8.9 23.8 all-gather.8
  34.4 30.6 all-gather.4
  66.7 36.0 all-gather.10
  104.2 22.7 all-gather.6
where the time goes:
time: 144 us; the launch traced here: 142 us
  waiting for transfers between devices  105 us (73%)
  between operations  13.3 us (9%)
  matrix products  11.6 us (8%)
  blocking collectives  9.87 us (7%)
    all_gather x1, waiting for transfers between devices, local(): full_tokens = lax.all_gather(tokens, 'head', axis=1, tiled=True)  32.4 us
    all_gather x1, waiting for transfers between devices, local(): lax.all_gather(query_frozen_matrix, 'ctx', axis=0, tiled=True)  28.9 us
    all_gather x1, waiting for transfers between devices, local(): key_base = add_rows(lax.all_gather(key_weight, 'ctx', axis=0, tiled=True))  22.1 us
    all_gather x1, waiting for transfers between devices, local(): lax.all_gather(value_frozen_matrix, 'ctx', axis=0, tiled=True)  18.9 us
    dot_general x3, matrix products, add_rows(): return jnp.dot(full_tokens, weight_part, preferred_element_type=jnp.float32)  7.33 us
    all_gather x1, blocking collectives, local(): lax.all_gather(key_proj, 'ctx', axis=0, tiled=True)  4.93 us
    all_gather x1, blocking collectives, local(): lax.all_gather(value_projected, 'ctx', axis=0, tiled=True)  4.93 us
  transfers between devices with their start and end apart: 4, of which 4 were waited for; matrix products, arithmetic and copies ran while one was open for 7% of the time, Pallas kernels for 0%

commit v1 on v0

--- a/solution.py
+++ b/solution.py
@@ -3,6 +3,8 @@
 import jax
 import jax.numpy as jnp
 from jax import lax
+from jax.experimental import pallas as pl
+from jax.experimental.pallas import tpu as pltpu
 from jax.sharding import PartitionSpec as P
 
 HD = 128
@@ -137,6 +139,221 @@
     return attended.reshape(tok_rows, local_heads * HD).astype(jnp.bfloat16)
 
 
+VMEM = pl.BlockSpec(memory_space=pltpu.VMEM)
+SMEM = pl.BlockSpec(memory_space=pltpu.SMEM)
+F32, BF16 = jnp.float32, jnp.bfloat16
+
+
+def call(body, outs, in_specs, flops, **kw):
+    multi = isinstance(outs, (list, tuple))
+    return pl.pallas_call(
+        body,
+        out_shape=outs,
+        in_specs=in_specs,
+        out_specs=[VMEM] * len(outs) if multi else VMEM,
+        cost_estimate=pl.CostEstimate(flops=flops, bytes_accessed=1 << 20, transcendentals=0),
+        compiler_params=pltpu.CompilerParams(vmem_limit_bytes=12 << 20),
+        **kw,
+    )
+
+
+def prep_body(q_ref, k_ref, v_ref, dq_ref, dv_ref, out_ref):
+    depth = out_ref.shape[2]
+    for b in range(out_ref.shape[0]):
+        at = 0
+        span = slice(b * depth, (b + 1) * depth)
+        for ref in (q_ref, k_ref, v_ref):
+            out_ref[b, at : at + ref.shape[1], :] = ref[span, :].T
+            at += ref.shape[1]
+        for ref in (dq_ref, dv_ref):
+            out_ref[b, at : at + ref.shape[0], :] = ref[:, span]
+            at += ref.shape[0]
+
+
+def dot(a, b):
+    return jnp.dot(a, b, preferred_element_type=F32)
+
+
+def first_body(ids_ref, w_ref, m0, m1, n0, n1, out_m, out_n):
+    own, twin = ids_ref[0], ids_ref[1]
+    out_m[...] = dot(w_ref[own], m0[...]) + dot(w_ref[twin], m1[...])
+    out_n[...] = dot(w_ref[own], n0[...]) + dot(w_ref[twin], n1[...])
+
+
+def second_body(wide_q, first_sent, ids_ref, w_ref, x0, x1, part, eq_ref, ev_ref, keep, send):
+    own, twin = ids_ref[2], ids_ref[3]
+    total = part[...] + dot(w_ref[own], x0[...]) + dot(w_ref[twin], x1[...])
+    rank = eq_ref.shape[1]
+    wide_v = ev_ref.shape[0]
+    wide = send.shape[0] + first_sent
+    low_q = total[wide : wide + rank].astype(BF16)
+    low_v = total[wide + rank : wide + 2 * rank].astype(BF16)
+    query = total[:wide_q] + dot(eq_ref[...], low_q)
+    key = total[wide_q : wide - wide_v]
+    value = total[wide - wide_v : wide] + dot(ev_ref[...], low_v)
+    keep[:wide_q] = query
+    keep[wide_q : wide - wide_v] = key
+    keep[wide - wide_v :] = value
+    if first_sent == 0:
+        send[:wide_q] = query.astype(BF16)
+    send[wide_q - first_sent : wide - wide_v - first_sent] = key.astype(BF16)
+    send[wide - wide_v - first_sent :] = value.astype(BF16)
+
+
+def turn(x, cos, sin):
+    half = x.shape[0] // 2
+    a, b = x[:half], x[half:]
+    return jnp.concatenate([a * cos - b * sin, b * cos + a * sin], axis=0)
+
+
+def attend_body(heads, mine, mine_in, other, other_in, cos_ref, sin_ref, vis_ref, out_ref):
+    rows = mine.shape[1]
+    wide_q = heads * HD
+    cos, sin = cos_ref[...], sin_ref[...]
+    cos_n, sin_n = cos[:, :rows], sin[:, :rows]
+    total = mine[...] + mine_in[...].astype(F32)
+    queries = jnp.concatenate(
+        [
+            (turn(total[h * HD : (h + 1) * HD], cos_n, sin_n) * query_scale).astype(BF16)
+            for h in range(heads)
+        ],
+        axis=1,
+    )
+    rest = other[wide_q:] + other_in[...].astype(F32)
+    keys = jnp.concatenate([total[wide_q : wide_q + HD], rest[:HD]], axis=1)
+    keys = turn(keys, cos, sin).astype(BF16)
+    values = jnp.concatenate(
+        [total[wide_q + HD :].astype(BF16), rest[HD:].astype(BF16)], axis=1
+    )
+    scores = dot(keys.T, queries)
+    capped = softcap_limit * jnp.tanh(scores / softcap_limit)
+    weights = jnp.exp(capped)
+    visible = vis_ref[...]
+    for h in range(heads):
+        w = weights[:, h * rows : (h + 1) * rows] * visible
+        denominator = jnp.sum(w, axis=0, keepdims=True)
+        numerator = dot(values, w.astype(BF16))
+        out_ref[:, h * HD : (h + 1) * HD] = (numerator / denominator).T.astype(BF16)
+
+
+def local_fast(
+    tokens,
+    query_frozen_matrix,
+    key_weight,
+    value_frozen_matrix,
+    query_down,
+    query_adapter_expand,
+    value_down,
+    value_adapter_expand,
+    block_order,
+    doc_starts,
+    prompt_of,
+):
+    rows, depth = tokens.shape
+    c, h = lax.axis_index("ctx"), lax.axis_index("head")
+    chips = lax.axis_size("head") // 2
+    sequence_len = rows * 2
+    z = h // 2
+    near = (z // 2) == c
+    both = ("ctx", "head")
+
+    def at(ci, zi, k):
+        return ci * chips * 2 + zi * 2 + k
+
+    q1_pairs, q2_pairs, z_pairs, zf_pairs = [], [], [], []
+    for ci in range(2):
+        for zi in range(chips):
+            for k in range(2):
+                me = at(ci, zi, k)
+                z_pairs.append((me, at(ci, zi ^ 1, k)))
+                if zi // 2 == ci:
+                    q1_pairs.append((me, at(ci, zi ^ 2, k)))
+                    q2_pairs.append((me, at(ci, zi ^ 1, k)))
+                else:
+                    q1_pairs.append((me, at(1 - ci, zi, k)))
+                    q2_pairs.append((me, at(1 - ci, zi ^ 2, k)))
+                    zf_pairs.append((me, at(ci, zi ^ 1, k)))
+    core = [(i, i ^ 1) for i in range(chips * 2)]
+
+    def send(x, pairs):
+        return lax.ppermute(x, both, pairs)
+
+    def twin(x):
+        return lax.ppermute(x, "head", core)
+
+    own = tokens.T
+    q1 = send(own, q1_pairs)
+    q2 = send(own, q2_pairs)
+    other_a = jnp.where(near, q1, q2)
+    mine_a = jnp.where(near, own, q1)
+    other_b = send(other_a, z_pairs)
+    late = send(q1, zf_pairs)
+    mine_b = jnp.where(near, q2, late)
+
+    own_ids = c * rows + jnp.arange(rows, dtype=jnp.int32)
+    key_ids = jnp.concatenate([own_ids, (1 - c) * rows + jnp.arange(rows, dtype=jnp.int32)])
+    info = lambda ids: row_meta(ids, block_order, doc_starts, prompt_of, rows // 2, sequence_len)
+    own_info, key_info = info(own_ids), info(key_ids)
+    visible = visible_mask(own_info, key_info).T.astype(F32)
+    frequency = jnp.exp(
+        jnp.arange(HD // 2, dtype=F32) * (-2.0 * math.log(rope_base) / HD)
+    )
+    angles = frequency[:, None] * key_info[3].astype(F32)[None, :]
+    cos, sin = jnp.cos(angles), jnp.sin(angles)
+
+    wide_q, wide_kv = query_frozen_matrix.shape[1], key_weight.shape[1]
+    wide = wide_q + 2 * wide_kv
+    rank = query_down.shape[1]
+    half = query_frozen_matrix.shape[0]
+    parts = half // depth
+    down_q = lax.dynamic_slice_in_dim(query_down.T, c * half, half, axis=1)
+    down_v = lax.dynamic_slice_in_dim(value_down.T, c * half, half, axis=1)
+    expand_q = (adapter_scaling * query_adapter_expand).astype(BF16).T
+    expand_v = (adapter_scaling * value_adapter_expand).astype(BF16).T
+    weights = call(
+        prep_body,
+        jax.ShapeDtypeStruct((parts, wide + 2 * rank, depth), BF16),
+        [VMEM] * 5,
+        10**9,
+    )(query_frozen_matrix, key_weight, value_frozen_matrix, down_q, down_v)
+
+    k = h % 2
+    par = (z % 2) * 2
+    ids = jnp.stack([par + k, par + 1 - k, 2 - par + k, 3 - par - k]).astype(jnp.int32)
+
+    whole = jax.ShapeDtypeStruct((wide + 2 * rank, rows), F32)
+    kept = jax.ShapeDtypeStruct((wide, rows), F32)
+    part_m, part_n = call(first_body, [whole, whole], [SMEM] + [VMEM] * 5, 10**9)(
+        ids, weights, other_a, twin(other_a), mine_a, twin(mine_a)
+    )
+
+    def second(first_sent):
+        def body(*refs):
+            second_body(wide_q, first_sent, *refs)
+
+        outs = [kept, jax.ShapeDtypeStruct((wide - first_sent, rows), BF16)]
+        return call(body, outs, [SMEM] + [VMEM] * 6, 5 * 10**8)
+
+    other_keep, other_send = second(0)(
+        ids, weights, other_b, twin(other_b), part_m, expand_q, expand_v
+    )
+    swap = [(0, 1), (1, 0)]
+    mine_in = lax.ppermute(other_send, "ctx", swap)
+    mine_keep, mine_send = second(wide_q)(
+        ids, weights, mine_b, twin(mine_b), part_n, expand_q, expand_v
+    )
+    other_in = lax.ppermute(mine_send, "ctx", swap)
+
+    heads = wide_q // HD
+
+    def last(*refs):
+        attend_body(heads, *refs)
+
+    return call(last, jax.ShapeDtypeStruct((rows, wide_q), BF16), [VMEM] * 7, 10**9)(
+        mine_keep, mine_in, other_keep, other_in, cos, sin, visible
+    )
+
+
 def solution(mesh):
     in_specs = (
         P(("tenant", "ctx"), "head"),
@@ -152,4 +369,6 @@
         P("tenant"),
     )
     out_specs = P(("tenant", "ctx"), "head")
-    return jax.shard_map(local, mesh=mesh, in_specs=in_specs, out_specs=out_specs, check_vma=False)
+    fits = mesh.shape["ctx"] == 2 and mesh.shape["head"] == 8
+    body = local_fast if fits else local
+    return jax.shard_map(body, mesh=mesh, in_specs=in_specs, out_specs=out_specs, check_vma=False)

time: 144 us -> 55.8 us (0.39); the launches traced: 142 us -> 55.4 us
  waiting for transfers between devices: 105 us -> 21.3 us
  starting transfers between devices: 0.15 us -> 14.4 us
  between operations: 13.3 us -> 0.21 us
  matrix products: 11.6 us -> 0 us
  blocking collectives: 9.87 us -> 0 us
  Pallas kernels: 0 us -> 8.19 us
  other arithmetic: 1.36 us -> 9.43 us
    all_gather x4 -> x0, waiting for transfers between devices: 102 us -> none  [the longest x1 32.4 us: local(): full_tokens = lax.all_gather(tokens, 'head', axis=1, tiled=True)]
    ppermute x0 -> x10, waiting for transfers between devices: none -> 21.3 us  [the longest x4 14.2 us: send(): return lax.ppermute(x, both, pairs)]
    ppermute x0 -> x10, starting transfers between devices: none -> 14.4 us  [the longest x4 11.7 us: send(): return lax.ppermute(x, both, pairs)]
    dot_general x7 -> x0, matrix products: 11.6 us -> none  [the longest x3 7.33 us: add_rows(): return jnp.dot(full_tokens, weight_part, preferred_element_type=jnp.float32)]
    all_gather x2 -> x0, blocking collectives: 9.87 us -> none  [the longest x1 4.93 us: local(): lax.all_gather(key_proj, 'ctx', axis=0, tiled=True)]
    pallas_call x0 -> x5, Pallas kernels: none -> 8.19 us  [the longest x1 2.19 us: local_fast(): call(first_body, [whole, whole], [SMEM] + [VMEM] * 5, 10 ** 9)]
    unnamed x4 -> x0, waiting for transfers between devices: 2.58 us -> none
    select_n x0 -> x1, other arithmetic: none -> 1.73 us  [local_fast(): mine_a = jnp.where(near, own, q1)]
  transfers between devices with their start and end apart: 4 -> 10, of which waited for: 4 -> 4; matrix products, arithmetic and copies ran while one was open for 7% -> 17% of each run, Pallas kernels for 0% -> 12%
where the time goes in v1:
time: 55.8 us; the launch traced here: 55.4 us
  waiting for transfers between devices  21.3 us (38%)
  starting transfers between devices  14.4 us (26%)
  other arithmetic  9.43 us (17%)
  Pallas kernels  8.19 us (15%)
  local copies, waits for them, and re-layouts  1.94 us (3%)
    ppermute x4, waiting for transfers between devices, send(): return lax.ppermute(x, both, pairs)  14.2 us
    ppermute x4, starting transfers between devices, send(): return lax.ppermute(x, both, pairs)  11.7 us
    ppermute x1, waiting for transfers between devices, local_fast(): other_in = lax.ppermute(mine_send, 'ctx', swap)  7.06 us
    pallas_call x1, Pallas kernels, local_fast(): call(first_body, [whole, whole], [SMEM] + [VMEM] * 5, 10 ** 9)  2.19 us
    ppermute x1, starting transfers between devices, local_fast(): other_in = lax.ppermute(mine_send, 'ctx', swap)  2.01 us
    pallas_call x1, Pallas kernels, local_fast(): second(0)(ids, weights, other_b, twin(other_b), part_m, expand_q, expand_v)  1.91 us
    pallas_call x1, Pallas kernels, local_fast(): second(wide_q)  1.88 us
    select_n x1, other arithmetic, local_fast(): mine_a = jnp.where(near, own, q1)  1.73 us
  transfers between devices with their start and end apart: 10, of which 4 were waited for; matrix products, arithmetic and copies ran while one was open for 17% of the time, Pallas kernels for 12%

profile of v1, /device:TPU:16, one launch (start us, length us, event | category | flops | bytes accessed | tf_op | source)
XLA Modules:
  0.0 55.4 jit_solution(4044950335248870021)
XLA Ops:
  0.0 1.5 %collective-permute-start.1 = (bf16[576,256]{1,0:T(8,128)(2,1)}, bf16[576,256]{1,0:T(8,128)(2,1)S(1)}, u32[]{:S(2)}, u32[]{:S(2)}) collective-permute-start(bf16[576,256]{1,0:T(8,128)(2,1)} %bitcast.16), channel_id=1, source_target_pairs={{0,4},{1,5},{2,6},{3,7},{4,12},{5,13},{6,14},{7,15},{8,0},{9,1},{1... | collective-permute-start | bytes 884744 | tf_op jit(solution)/shard_map/ppermute | solution.py:279
  1.5 0.7 %broadcast_multiply_fusion = bf16[16,256]{1,0:T(8,128)(2,1)S(1)} fusion(bf16[16,256]{1,0:T(8,128)(2,1)} %param.16), kind=kLoop, calls=%fused_computation.21 | loop fusion | flops 4096 | bytes 16384 | tf_op jit(solution)/shard_map/mul | solution.py:311
  2.2 0.7 %slice.3 = s32[11]{0:T(128)S(1)} slice(s32[12]{0:T(128)} %param.20), slice={[1:12]} | slice | bytes 88 | tf_op jit(solution)/shard_map/slice | solution.py:30
  3.0 0.7 %select_reduce_fusion.4 = s32[512]{0:T(512)S(1)} fusion(s32[4]{0:T(128)} %param.19, s32[512]{0:T(512)S(1)} %add_select_fusion.1), kind=kLoop, calls=%fused_computation.17 | loop fusion | flops 5632 | bytes 4112 | tf_op jit(solution)/shard_map/reduce_sum | solution.py:23
  3.7 0.7 %convert_reduce_fusion = s32[512]{0:T(512)S(1)} fusion(s32[512]{0:T(512)S(1)} %fusion, s32[12]{0:T(128)} %param.20), kind=kLoop, calls=%fused_computation.13 | loop fusion | flops 17920 | bytes 4144 | tf_op jit(solution)/shard_map/reduce_sum | solution.py:25
  4.5 0.7 %select_reduce_fusion.5 = s32[256]{0:T(256)S(1)} fusion(s32[4]{0:T(128)} %param.19, s32[256]{0:T(256)S(1)} %get-tuple-element.26), kind=kLoop, calls=%fused_computation.19 | loop fusion | flops 2816 | bytes 2064 | tf_op jit(solution)/shard_map/reduce_sum | solution.py:23
  5.2 0.7 %convert_reduce_fusion.1 = s32[256]{0:T(256)S(1)} fusion(s32[256]{0:T(256)S(1)} %fusion.2, s32[12]{0:T(128)} %param.20), kind=kLoop, calls=%fused_computation.16 | loop fusion | flops 8960 | bytes 2096 | tf_op jit(solution)/shard_map/reduce_sum | solution.py:25
  6.0 0.8 %select_reduce_fusion.2 = (s32[512]{0:T(512)S(1)}, s32[512]{0:T(512)S(1)}) fusion(s32[512]{0:T(512)S(1)} %broadcast_add_fusion, s32[12]{0:T(128)} %param.20, s32[12]{0:T(128)} %param.21), kind=kLoop, calls=%fused_computation.11 | loop fusion | flops 29696 | bytes 6240 | tf_op jit(solution)/shard_map/reduce_sum | solution.py:29
  6.7 0.7 %select_reduce_fusion.3 = s32[256]{0:T(256)S(1)} fusion(s32[12]{0:T(128)} %param.21, s32[256]{0:T(256)S(1)} %broadcast_add_fusion.1), kind=kLoop, calls=%fused_computation.14 | loop fusion | flops 8960 | bytes 2096 | tf_op jit(solution)/shard_map/reduce_sum | solution.py:28
  7.5 0.7 %add_subtract_fusion = s32[12]{0:T(128)S(1)} fusion(s32[12]{0:T(128)} %param.20, s32[1]{0:T(128)} %constant.110.clone.1, s32[11]{0:T(128)S(1)} %slice.3), kind=kLoop, calls=%fused_computation.45 | loop fusion | flops 24 | bytes 144 | tf_op jit(solution)/shard_map/sub | solution.py:32
  8.2 0.1 select_reduce_fusion
  8.4 1.0 %or_convert_fusion.refs_6_ = f32[512,256]{1,0:T(8,128)} fusion(s32[256]{0:T(256)S(1)} %select_reduce_fusion.3, s32[256]{0:T(256)S(1)} %fusion.2, s32[256]{0:T(256)S(1)} %broadcast_add_fusion.1, s32[512]{0:T(512)S(1)} %fusion, s32[512]{0:T(512)S(1)} %broadcast_add_fusion, pred[256]{0:T(512)(128)(4,1)S(1)} %fusion.4), kind=kLoop, calls=%fused_computation | loop fusion | flops 917504 | bytes 531712 | tf_op jit(solution)/shard_map/convert_element_type | solution.py:297
  9.4 1.6 %collective-permute-done.1 = bf16[576,256]{1,0:T(8,128)(2,1)S(1)} collective-permute-done((bf16[576,256]{1,0:T(8,128)(2,1)}, bf16[576,256]{1,0:T(8,128)(2,1)S(1)}, u32[]{:S(2)}, u32[]{:S(2)}) %collective-permute-start.1) | collective-permute-done | bytes 294944 | tf_op jit(solution)/shard_map/ppermute | solution.py:279
  11.0 8.5 %collective-permute-start.2 = (bf16[576,256]{1,0:T(8,128)(2,1)S(1)}, bf16[576,256]{1,0:T(8,128)(2,1)S(1)}, u32[]{:S(2)}, u32[]{:S(2)}) collective-permute-start(bf16[576,256]{1,0:T(8,128)(2,1)S(1)} %collective-permute-done.1), channel_id=1, source_target_pairs={{4,6},{5,7},{6,4},{7,5},{8,10},{9,11},{10,8},{11,9},{20,22},{21,23... | collective-permute-start | bytes 884744 | tf_op jit(solution)/shard_map/ppermute | solution.py:279
  19.5 0.9 %dynamic-slice_bitcast_fusion = (bf16[16,2304]{1,0:T(8,128)(2,1)S(1)}, bf16[16,2304]{1,0:T(8,128)(2,1)S(1)}) fusion(bf16[4608,16]{0,1:T(8,128)(2,1)} %param.17, s32[]{:T(128)S(6)} %select_n.116, bf16[4608,16]{0,1:T(8,128)(2,1)} %param.15), kind=kLoop, calls=%fused_computation.6 | loop fusion | bytes 294916 | tf_op jit(solution)/shard_map/dynamic_slice | solution.py:310
  20.5 6.2 %collective-permute-done.2 = bf16[576,256]{1,0:T(8,128)(2,1)S(1)} collective-permute-done((bf16[576,256]{1,0:T(8,128)(2,1)S(1)}, bf16[576,256]{1,0:T(8,128)(2,1)S(1)}, u32[]{:S(2)}, u32[]{:S(2)}) %collective-permute-start.2) | collective-permute-done | bytes 294944 | tf_op jit(solution)/shard_map/ppermute | solution.py:279
  26.7 1.7 %broadcast_select_fusion = (bf16[576,256]{1,0:T(8,128)(2,1)S(1)}, bf16[576,256]{1,0:T(8,128)(2,1)}, bf16[576,256]{1,0:T(8,128)(2,1)S(1)}) fusion(bf16[576,256]{1,0:T(8,128)(2,1)S(1)} %collective-permute-done.1, pred[]{:T(512)S(6)} %eq.50, bf16[256,576]{0,1:T(8,128)(2,1)} %param.11, bf16[576,256]{1,0:T(8,128)(2,1)S(1)} %collective-permute-done, ...), kind=kLoop, calls=%fused_computation.1 | loop fusion | flops 442368 | bytes 2064385 | tf_op jit(solution)/shard_map/jit(_where)/select_n | solution.py:288
  28.5 1.7 %collective-permute-start.6 = (bf16[576,256]{1,0:T(8,128)(2,1)}, bf16[576,256]{1,0:T(8,128)(2,1)}, u32[]{:S(2)}, u32[]{:S(2)}) collective-permute-start(bf16[576,256]{1,0:T(8,128)(2,1)} %get-tuple-element.20.m0), channel_id=1, source_target_pairs={{0,2},{1,3},{2,0},{3,1},{4,6},{5,7},{6,4},{7,5},{8,10},{9,11},{10,... | collective-permute-start | bytes 884744 | tf_op jit(solution)/shard_map/ppermute | solution.py:279
  30.2 0.5 collective-permute-start.5
  30.7 0.1 collective-permute-start.3
  30.8 6.3 %collective-permute-done.6.refs_2_ = bf16[576,256]{1,0:T(8,128)(2,1)} collective-permute-done((bf16[576,256]{1,0:T(8,128)(2,1)}, bf16[576,256]{1,0:T(8,128)(2,1)}, u32[]{:S(2)}, u32[]{:S(2)}) %collective-permute-start.6) | collective-permute-done | bytes 294944 | tf_op jit(solution)/shard_map/ppermute | solution.py:279
  37.1 0.8 %shard_map.109.w_ref.refs_1_ = bf16[4,544,576]{2,1,0:T(8,128)(2,1)S(1)} custom-call(bf16[2304,256]{1,0:T(8,128)(2,1)S(1)} %copy-done, bf16[2304,128]{1,0:T(8,128)(2,1)S(1)} %copy-done.1, bf16[2304,128]{1,0:T(8,128)(2,1)S(1)} %copy-done.2, bf16[16,2304]{1,0:T(8,128)(2,1)S(1)} %get-tuple-element.25.dq_ref, bf16[16,2304]{1,0:T(8,128)(2,1)S(1)} %get-tuple-element.24.dv_ref), custom_call_target="tpu_custom_call" | custom-call | flops 1000000000 | bytes 1048576 | tf_op jit(solution)/shard_map/pallas_call | solution.py:313
  38.0 0.1 copy.20
  38.1 0.1 copy.21
  38.2 0.1 pad_add_fusion.1.ids_ref.refs_0_
  38.3 2.2 %shard_map.110 = (f32[544,256]{1,0:T(8,128)S(1)}, f32[544,256]{1,0:T(8,128)S(1)}) custom-call(s32[4]{0:T(128)S(1)} %pad_add_fusion.1.ids_ref.refs_0_, bf16[4,544,576]{2,1,0:T(8,128)(2,1)S(1)} %shard_map.109.w_ref.refs_1_, bf16[576,256]{1,0:T(8,128)(2,1)} %get-tuple-element.20.m0, bf16[576,256]{1,0:T(8,128)(2,1)} %collective-permute-done.4.m1, ...), custom_call_target="tpu_custom_call" | custom-call | flops 1000000000 | bytes 1048576 | tf_op jit(solution)/shard_map/pallas_call | solution.py:326
  40.5 1.9 %shard_map.112 = (f32[512,256]{1,0:T(8,128)S(1)}, bf16[512,256]{1,0:T(8,128)(2,1)S(1)}) custom-call(s32[4]{0:T(128)S(1)} %pad_add_fusion.1.ids_ref.refs_0_, bf16[4,544,576]{2,1,0:T(8,128)(2,1)S(1)} %shard_map.109.w_ref.refs_1_, bf16[576,256]{1,0:T(8,128)(2,1)} %collective-permute-done.6.refs_2_, bf16[576,256]{1,0:T(8,128)(2,1)} %collective-permute-done.7.refs_3_, ...), custom_call_target="tpu_custom_call" | custom-call | flops 500000000 | bytes 1048576 | tf_op jit(solution)/shard_map/pallas_call | solution.py:337
  42.5 1.9 %shard_map.111 = (f32[512,256]{1,0:T(8,128)S(1)}, bf16[256,256]{1,0:T(8,128)(2,1)S(1)}) custom-call(s32[4]{0:T(128)S(1)} %pad_add_fusion.1.ids_ref.refs_0_, bf16[4,544,576]{2,1,0:T(8,128)(2,1)S(1)} %shard_map.109.w_ref.refs_1_, bf16[576,256]{1,0:T(8,128)(2,1)S(1)} %get-tuple-element.21.refs_2_, bf16[576,256]{1,0:T(8,128)(2,1)} %collective-permute-done.3.refs_3_, ...), custom_call_target="tpu_custom_call" | custom-call | flops 500000000 | bytes 1048576 | tf_op jit(solution)/shard_map/pallas_call | solution.py:342
  44.4 2.0 %collective-permute-start.9 = (bf16[256,256]{1,0:T(8,128)(2,1)S(1)}, bf16[256,256]{1,0:T(8,128)(2,1)S(1)}, u32[]{:S(2)}, u32[]{:S(2)}) collective-permute-start(bf16[256,256]{1,0:T(8,128)(2,1)S(1)} %get-tuple-element.16), channel_id=1, source_target_pairs={{0,8},{8,0},{1,9},{9,1},{2,10},{10,2},{3,11},{11,3},{4,12},{12,4},... | collective-permute-start | bytes 393224 | tf_op jit(solution)/shard_map/ppermute | solution.py:345
  46.4 0.5 multiply_sine_fusion
  47.0 7.1 %collective-permute-done.9.refs_3_ = bf16[256,256]{1,0:T(8,128)(2,1)S(1)} collective-permute-done((bf16[256,256]{1,0:T(8,128)(2,1)S(1)}, bf16[256,256]{1,0:T(8,128)(2,1)S(1)}, u32[]{:S(2)}, u32[]{:S(2)}) %collective-permute-start.9) | collective-permute-done | bytes 131104 | tf_op jit(solution)/shard_map/ppermute | solution.py:345
  54.0 1.4 %shard_map.113 = bf16[256,256]{1,0:T(8,128)(2,1)} custom-call(f32[512,256]{1,0:T(8,128)S(1)} %get-tuple-element.12.refs_0_, bf16[512,256]{1,0:T(8,128)(2,1)S(1)} %collective-permute-done.8.refs_1_, f32[512,256]{1,0:T(8,128)S(1)} %get-tuple-element.15.refs_2_, bf16[256,256]{1,0:T(8,128)(2,1)S(1)} %collective-permute-done.9.refs_3_, ...), custom_call_target="tpu_custom_call" | custom-call | flops 1000000000 | bytes 1048576 | tf_op jit(solution)/shard_map/pallas_call | solution.py:352
  (31 shorter events, 0.2 us)
Async XLA Ops:
  0.0 30.2 %copy-start.4 = (bf16[16,128]{1,0:T(8,128)(2,1)S(1)}, bf16[16,128]{1,0:T(8,128)(2,1)}, u32[]{:S(2)}) copy-start(bf16[16,128]{1,0:T(8,128)(2,1)} %param.18) | copy-start | bytes 12292
  0.0 11.0 %collective-permute-start.1 = (bf16[576,256]{1,0:T(8,128)(2,1)}, bf16[576,256]{1,0:T(8,128)(2,1)S(1)}, u32[]{:S(2)}, u32[]{:S(2)}) collective-permute-start(bf16[576,256]{1,0:T(8,128)(2,1)} %bitcast.16), channel_id=1, source_target_pairs={{0,4},{1,5},{2,6},{3,7},{4,12},{5,13},{6,14},{7,15},{8,0},{9,1},{1... | collective-permute-start | bytes 884744 | tf_op jit(solution)/shard_map/ppermute | solution.py:279
  1.5 19.0 %collective-permute-start = (bf16[576,256]{1,0:T(8,128)(2,1)}, bf16[576,256]{1,0:T(8,128)(2,1)S(1)}, u32[]{:S(2)}, u32[]{:S(2)}) collective-permute-start(bf16[576,256]{1,0:T(8,128)(2,1)} %bitcast.17), channel_id=1, source_target_pairs={{0,2},{1,3},{2,0},{3,1},{4,8},{5,9},{6,10},{7,11},{8,4},{9,5},{10,... | collective-permute-start | bytes 884744 | tf_op jit(solution)/shard_map/ppermute | solution.py:279
  8.3 28.8 %copy-start = (bf16[2304,256]{1,0:T(8,128)(2,1)S(1)}, bf16[2304,256]{1,0:T(8,128)(2,1)}, u32[]{:S(2)}) copy-start(bf16[2304,256]{1,0:T(8,128)(2,1)} %q_ref.1) | copy-start | bytes 3538948
  8.4 28.8 %copy-start.1 = (bf16[2304,128]{1,0:T(8,128)(2,1)S(1)}, bf16[2304,128]{1,0:T(8,128)(2,1)}, u32[]{:S(2)}) copy-start(bf16[2304,128]{1,0:T(8,128)(2,1)} %k_ref.1) | copy-start | bytes 1769476
  8.4 28.8 %copy-start.2 = (bf16[2304,128]{1,0:T(8,128)(2,1)S(1)}, bf16[2304,128]{1,0:T(8,128)(2,1)}, u32[]{:S(2)}) copy-start(bf16[2304,128]{1,0:T(8,128)(2,1)} %v_ref.1) | copy-start | bytes 1769476
  11.0 15.7 %collective-permute-start.2 = (bf16[576,256]{1,0:T(8,128)(2,1)S(1)}, bf16[576,256]{1,0:T(8,128)(2,1)S(1)}, u32[]{:S(2)}, u32[]{:S(2)}) collective-permute-start(bf16[576,256]{1,0:T(8,128)(2,1)S(1)} %collective-permute-done.1), channel_id=1, source_target_pairs={{4,6},{5,7},{6,4},{7,5},{8,10},{9,11},{10,8},{11,9},{20,22},{21,23... | collective-permute-start | bytes 884744 | tf_op jit(solution)/shard_map/ppermute | solution.py:279
  28.5 8.7 %collective-permute-start.6 = (bf16[576,256]{1,0:T(8,128)(2,1)}, bf16[576,256]{1,0:T(8,128)(2,1)}, u32[]{:S(2)}, u32[]{:S(2)}) collective-permute-start(bf16[576,256]{1,0:T(8,128)(2,1)} %get-tuple-element.20.m0), channel_id=1, source_target_pairs={{0,2},{1,3},{2,0},{3,1},{4,6},{5,7},{6,4},{7,5},{8,10},{9,11},{10,... | collective-permute-start | bytes 884744 | tf_op jit(solution)/shard_map/ppermute | solution.py:279
  30.2 8.1 %collective-permute-start.4 = (bf16[576,256]{1,0:T(8,128)(2,1)}, bf16[576,256]{1,0:T(8,128)(2,1)}, u32[]{:S(2)}, u32[]{:S(2)}) collective-permute-start(bf16[576,256]{1,0:T(8,128)(2,1)} %get-tuple-element.20.m0), channel_id=1, source_target_pairs={{0,1},{1,0},{2,3},{3,2},{4,5},{5,4},{6,7},{7,6},{8,9},{9,8},{10,11... | collective-permute-start | bytes 884744 | tf_op jit(solution)/shard_map/ppermute | solution.py:282
  30.2 8.1 %collective-permute-start.5 = (bf16[576,256]{1,0:T(8,128)(2,1)S(1)}, bf16[576,256]{1,0:T(8,128)(2,1)}, u32[]{:S(2)}, u32[]{:S(2)}) collective-permute-start(bf16[576,256]{1,0:T(8,128)(2,1)S(1)} %get-tuple-element.19.n0), channel_id=1, source_target_pairs={{0,1},{1,0},{2,3},{3,2},{4,5},{5,4},{6,7},{7,6},{8,9},{9,8},{10,11... | collective-permute-start | bytes 884744 | tf_op jit(solution)/shard_map/ppermute | solution.py:282
  30.7 11.8 %collective-permute-start.3 = (bf16[576,256]{1,0:T(8,128)(2,1)S(1)}, bf16[576,256]{1,0:T(8,128)(2,1)}, u32[]{:S(2)}, u32[]{:S(2)}) collective-permute-start(bf16[576,256]{1,0:T(8,128)(2,1)S(1)} %get-tuple-element.21.refs_2_), channel_id=1, source_target_pairs={{0,1},{1,0},{2,3},{3,2},{4,5},{5,4},{6,7},{7,6},{8,9},{9,8},{10,11... | collective-permute-start | bytes 884744 | tf_op jit(solution)/shard_map/ppermute | solution.py:282
  37.1 3.4 %collective-permute-start.7 = (bf16[576,256]{1,0:T(8,128)(2,1)}, bf16[576,256]{1,0:T(8,128)(2,1)}, u32[]{:S(2)}, u32[]{:S(2)}) collective-permute-start(bf16[576,256]{1,0:T(8,128)(2,1)} %collective-permute-done.6.refs_2_), channel_id=1, source_target_pairs={{0,1},{1,0},{2,3},{3,2},{4,5},{5,4},{6,7},{7,6},{8,9},{9,8},{10,11... | collective-permute-start | bytes 884744 | tf_op jit(solution)/shard_map/ppermute | solution.py:282
  42.4 11.6 %copy-start.3 = (f32[512,256]{1,0:T(8,128)S(1)}, f32[512,256]{1,0:T(8,128)}, u32[]{:S(2)}) copy-start(f32[512,256]{1,0:T(8,128)} %or_convert_fusion.refs_6_) | copy-start | bytes 1572868
  42.4 11.6 %collective-permute-start.8 = (bf16[512,256]{1,0:T(8,128)(2,1)S(1)}, bf16[512,256]{1,0:T(8,128)(2,1)S(1)}, u32[]{:S(2)}, u32[]{:S(2)}) collective-permute-start(bf16[512,256]{1,0:T(8,128)(2,1)S(1)} %get-tuple-element.14), channel_id=1, source_target_pairs={{0,8},{8,0},{1,9},{9,1},{2,10},{10,2},{3,11},{11,3},{4,12},{12,4},... | collective-permute-start | bytes 786440 | tf_op jit(solution)/shard_map/ppermute | solution.py:341
  44.4 9.6 %collective-permute-start.9 = (bf16[256,256]{1,0:T(8,128)(2,1)S(1)}, bf16[256,256]{1,0:T(8,128)(2,1)S(1)}, u32[]{:S(2)}, u32[]{:S(2)}) collective-permute-start(bf16[256,256]{1,0:T(8,128)(2,1)S(1)} %get-tuple-element.16), channel_id=1, source_target_pairs={{0,8},{8,0},{1,9},{9,1},{2,10},{10,2},{3,11},{11,3},{4,12},{12,4},... | collective-permute-start | bytes 393224 | tf_op jit(solution)/shard_map/ppermute | solution.py:345

commit v2 on v1

--- a/solution.py
+++ b/solution.py
@@ -6,6 +6,7 @@
 from jax.experimental import pallas as pl
 from jax.experimental.pallas import tpu as pltpu
 from jax.sharding import PartitionSpec as P
+
 
 HD = 128
 
@@ -198,6 +199,16 @@
         send[:wide_q] = query.astype(BF16)
     send[wide_q - first_sent : wide - wide_v - first_sent] = key.astype(BF16)
     send[wide - wide_v - first_sent :] = value.astype(BF16)
+
+
+def pick_body(flag_ref, a_ref, b_ref, out_ref):
+    @pl.when(flag_ref[0] == 1)
+    def _():
+        out_ref[...] = a_ref[...]
+
+    @pl.when(flag_ref[0] != 1)
+    def _():
+        out_ref[...] = b_ref[...]
 
 
 def turn(x, cos, sin):
@@ -284,11 +295,6 @@
     own = tokens.T
     q1 = send(own, q1_pairs)
     q2 = send(own, q2_pairs)
-    other_a = jnp.where(near, q1, q2)
-    mine_a = jnp.where(near, own, q1)
-    other_b = send(other_a, z_pairs)
-    late = send(q1, zf_pairs)
-    mine_b = jnp.where(near, q2, late)
 
     own_ids = c * rows + jnp.arange(rows, dtype=jnp.int32)
     key_ids = jnp.concatenate([own_ids, (1 - c) * rows + jnp.arange(rows, dtype=jnp.int32)])
@@ -323,9 +329,25 @@
 
     whole = jax.ShapeDtypeStruct((wide + 2 * rank, rows), F32)
     kept = jax.ShapeDtypeStruct((wide, rows), F32)
+    flag = near.astype(jnp.int32)[None]
+    tables = (weights, ids, flag, expand_q, expand_v, visible)
+    q1, q2, tables = lax.optimization_barrier((q1, q2, tables))
+    weights, ids, flag, expand_q, expand_v, visible = tables
+
+    def pick(a, b):
+        out = jax.ShapeDtypeStruct(a.shape, a.dtype)
+        return call(pick_body, out, [SMEM, VMEM, VMEM], 10**7)(flag, a, b)
+
+    other_a = pick(q1, q2)
+    other_b = send(other_a, z_pairs)
+    late = send(q1, zf_pairs)
+    mine_a = pick(own, q1)
+    other_a_twin = twin(other_a)
+    mine_a_twin = twin(mine_a)
     part_m, part_n = call(first_body, [whole, whole], [SMEM] + [VMEM] * 5, 10**9)(
-        ids, weights, other_a, twin(other_a), mine_a, twin(mine_a)
-    )
+        ids, weights, other_a, other_a_twin, mine_a, mine_a_twin
+    )
+    mine_b = pick(q2, late)
 
     def second(first_sent):
         def body(*refs):
@@ -370,5 +392,12 @@
     )
     out_specs = P(("tenant", "ctx"), "head")
     fits = mesh.shape["ctx"] == 2 and mesh.shape["head"] == 8
-    body = local_fast if fits else local
-    return jax.shard_map(body, mesh=mesh, in_specs=in_specs, out_specs=out_specs, check_vma=False)
+
+    def body(*args):
+        if not fits:
+            return local(*args)
+        return local_fast(*args)
+
+    return jax.shard_map(
+        body, mesh=mesh, in_specs=in_specs, out_specs=out_specs, check_vma=False
+    )

time: 55.8 us -> 51.8 us (0.928)
  local copies, waits for them, and re-layouts: 1.94 us -> 5.32 us
  starting transfers between devices: 14.4 us -> 11.7 us
  other arithmetic: 9.43 us -> 6.95 us
  Pallas kernels: 8.19 us -> 6.68 us
  waiting for transfers between devices: 21.3 us -> 20.4 us
    unnamed x10, local copies, waits for them, and re-layouts: 0.03 us -> 3.41 us
    ppermute x4, starting transfers between devices: 11.7 us -> 8.89 us  [send(): return lax.ppermute(x, both, pairs)]
    select_n x1 -> x0, other arithmetic: 1.73 us -> none  [local_fast(): mine_a = jnp.where(near, own, q1)]
    ppermute x4, waiting for transfers between devices: 14.2 us -> 12.9 us  [send(): return lax.ppermute(x, both, pairs)]
    convert_element_type x1, other arithmetic: 1.01 us -> 0.22 us  [local_fast(): visible = visible_mask(own_info, key_info).T.astype(F32)]
    mul x1, other arithmetic: 0.01 us -> 0.69 us  [local_fast(): expand_v = (adapter_scaling * value_adapter_expand).astype(BF16).T]
    sub x1, other arithmetic: 0.73 us -> 0.08 us  [row_meta(): next_starts - doc_starts]
    pallas_call x1, Pallas kernels: 2.19 us -> 1.58 us  [local_fast(): call(first_body, [whole, whole], [SMEM] + [VMEM] * 5, 10 ** 9)]
  transfers between devices with their start and end apart: 10 -> 10, of which waited for: 4 -> 4; matrix products, arithmetic and copies ran while one was open for 17% -> 17% of each run, Pallas kernels for 12% -> 10%
where the time goes in v2:
time: 51.8 us; the launch traced here: 51.2 us
  waiting for transfers between devices  20.4 us (39%)
  starting transfers between devices  11.7 us (23%)
  other arithmetic  6.95 us (13%)
  Pallas kernels  6.68 us (13%)
  local copies, waits for them, and re-layouts  5.32 us (10%)
    ppermute x4, waiting for transfers between devices, send(): return lax.ppermute(x, both, pairs)  12.9 us
    ppermute x4, starting transfers between devices, send(): return lax.ppermute(x, both, pairs)  8.89 us
    ppermute x1, waiting for transfers between devices, local_fast(): other_in = lax.ppermute(mine_send, 'ctx', swap)  7.48 us
    unnamed x10, local copies, waits for them, and re-layouts  3.41 us
    ppermute x1, starting transfers between devices, local_fast(): other_in = lax.ppermute(mine_send, 'ctx', swap)  2.07 us
    pallas_call x1, Pallas kernels, local_fast(): call(first_body, [whole, whole], [SMEM] + [VMEM] * 5, 10 ** 9)  1.58 us
    reduce_sum x2, other arithmetic, row_meta(): jnp.sum((doc_starts[None, :] <= places[:, None]).astype(jnp.int32), axis=1)  1.48 us
    reduce_sum x2, other arithmetic, row_meta(): ordered = jnp.sum(jnp.where(one_hot, block_order[None, :], 0), axis=1)  1.48 us
  transfers between devices with their start and end apart: 10, of which 4 were waited for; matrix products, arithmetic and copies ran while one was open for 17% of the time, Pallas kernels for 10%

profile of v2, /device:TPU:16, one launch (start us, length us, event | category | flops | bytes accessed | tf_op | source)
XLA Modules:
  0.0 51.2 jit_solution(4908523227365353938)
XLA Ops:
  0.0 1.5 %collective-permute-start = (bf16[576,256]{1,0:T(8,128)(2,1)}, bf16[576,256]{1,0:T(8,128)(2,1)S(1)}, u32[]{:S(2)}, u32[]{:S(2)}) collective-permute-start(bf16[576,256]{1,0:T(8,128)(2,1)} %bitcast.16), channel_id=1, source_target_pairs={{0,4},{1,5},{2,6},{3,7},{4,12},{5,13},{6,14},{7,15},{8,0},{9,1},{1... | collective-permute-start | bytes 884744 | tf_op jit(solution)/shard_map/ppermute | solution.py:290
  1.5 0.7 %broadcast_multiply_fusion = bf16[16,256]{1,0:T(8,128)(2,1)S(1)} fusion(bf16[16,256]{1,0:T(8,128)(2,1)} %param.16), kind=kLoop, calls=%fused_computation.18 | loop fusion | flops 4096 | bytes 16384 | tf_op jit(solution)/shard_map/mul | solution.py:317
  2.2 0.1 copy.20
  2.3 0.7 %broadcast_multiply_fusion.1 = bf16[16,128]{1,0:T(8,128)(2,1)S(1)} fusion(bf16[16,128]{1,0:T(8,128)(2,1)} %param.18), kind=kLoop, calls=%fused_computation.28 | loop fusion | flops 2048 | bytes 8192 | tf_op jit(solution)/shard_map/mul | solution.py:318
  3.0 0.1 copy.21
  3.1 0.7 %select_reduce_fusion.5 = s32[256]{0:T(256)S(1)} fusion(s32[4]{0:T(128)} %param.19, s32[256]{0:T(256)S(1)} %get-tuple-element.39), kind=kLoop, calls=%fused_computation.16 | loop fusion | flops 2816 | bytes 2064 | tf_op jit(solution)/shard_map/reduce_sum | solution.py:24
  3.9 0.7 %slice.3 = s32[11]{0:T(128)S(1)} slice(s32[12]{0:T(128)} %param.20), slice={[1:12]} | slice | bytes 88 | tf_op jit(solution)/shard_map/slice | solution.py:31
  4.6 0.7 %convert_reduce_fusion.1 = s32[256]{0:T(256)S(1)} fusion(s32[256]{0:T(256)S(1)} %fusion.2, s32[12]{0:T(128)} %param.20), kind=kLoop, calls=%fused_computation.13 | loop fusion | flops 8960 | bytes 2096 | tf_op jit(solution)/shard_map/reduce_sum | solution.py:26
  5.4 0.7 %select_reduce_fusion.4 = s32[512]{0:T(512)S(1)} fusion(s32[4]{0:T(128)} %param.19, s32[512]{0:T(512)S(1)} %add_select_fusion.1), kind=kLoop, calls=%fused_computation.14 | loop fusion | flops 5632 | bytes 4112 | tf_op jit(solution)/shard_map/reduce_sum | solution.py:24
  6.2 0.7 %convert_reduce_fusion = s32[512]{0:T(512)S(1)} fusion(s32[512]{0:T(512)S(1)} %fusion, s32[12]{0:T(128)} %param.20), kind=kLoop, calls=%fused_computation.10 | loop fusion | flops 17920 | bytes 4144 | tf_op jit(solution)/shard_map/reduce_sum | solution.py:26
  6.9 0.7 %select_reduce_fusion.3 = s32[256]{0:T(256)S(1)} fusion(s32[12]{0:T(128)} %param.21, s32[256]{0:T(256)S(1)} %broadcast_add_fusion.1), kind=kLoop, calls=%fused_computation.11 | loop fusion | flops 8960 | bytes 2096 | tf_op jit(solution)/shard_map/reduce_sum | solution.py:29
  7.7 0.8 %select_reduce_fusion.2 = (s32[512]{0:T(512)S(1)}, s32[512]{0:T(512)S(1)}) fusion(s32[512]{0:T(512)S(1)} %broadcast_add_fusion, s32[12]{0:T(128)} %param.20, s32[12]{0:T(128)} %param.21), kind=kLoop, calls=%fused_computation.8 | loop fusion | flops 29696 | bytes 6240 | tf_op jit(solution)/shard_map/reduce_sum | solution.py:30
  8.4 0.9 %dynamic-slice_bitcast_fusion = (bf16[16,2304]{1,0:T(8,128)(2,1)S(1)}, bf16[16,2304]{1,0:T(8,128)(2,1)S(1)}) fusion(bf16[4608,16]{0,1:T(8,128)(2,1)} %param.17, s32[]{:T(128)S(6)} %select_n.97, bf16[4608,16]{0,1:T(8,128)(2,1)} %param.15), kind=kLoop, calls=%fused_computation.3 | loop fusion | bytes 294916 | tf_op jit(solution)/shard_map/dynamic_slice | solution.py:316
  9.4 0.1 pad_add_fusion.1.ids_ref.refs_0_
  9.5 1.3 %copy-done = bf16[2304,256]{1,0:T(8,128)(2,1)S(1)} copy-done((bf16[2304,256]{1,0:T(8,128)(2,1)S(1)}, bf16[2304,256]{1,0:T(8,128)(2,1)}, u32[]{:S(2)}) %copy-start) | copy-done | bytes 1179672
  10.7 1.1 %copy-done.1 = bf16[2304,128]{1,0:T(8,128)(2,1)S(1)} copy-done((bf16[2304,128]{1,0:T(8,128)(2,1)S(1)}, bf16[2304,128]{1,0:T(8,128)(2,1)}, u32[]{:S(2)}) %copy-start.1) | copy-done | bytes 589848
  11.8 1.1 %copy-done.2 = bf16[2304,128]{1,0:T(8,128)(2,1)S(1)} copy-done((bf16[2304,128]{1,0:T(8,128)(2,1)S(1)}, bf16[2304,128]{1,0:T(8,128)(2,1)}, u32[]{:S(2)}) %copy-start.2) | copy-done | bytes 589848
  12.9 0.8 %shard_map.109.w_ref.refs_1_ = bf16[4,544,576]{2,1,0:T(8,128)(2,1)S(1)} custom-call(bf16[2304,256]{1,0:T(8,128)(2,1)S(1)} %copy-done, bf16[2304,128]{1,0:T(8,128)(2,1)S(1)} %copy-done.1, bf16[2304,128]{1,0:T(8,128)(2,1)S(1)} %copy-done.2, bf16[16,2304]{1,0:T(8,128)(2,1)S(1)} %get-tuple-element.38.dq_ref, bf16[16,2304]{1,0:T(8,128)(2,1)S(1)} %get-tuple-element.37.dv_ref), custom_call_target="tpu_custom_call" | custom-call | flops 1000000000 | bytes 1048576 | tf_op jit(solution)/shard_map/pallas_call | solution.py:319
  13.7 0.2 or_convert_fusion.refs_6_
  13.9 0.5 %collective-permute-done.1.a_ref.b_ref = bf16[576,256]{1,0:T(8,128)(2,1)S(1)} collective-permute-done((bf16[576,256]{1,0:T(8,128)(2,1)}, bf16[576,256]{1,0:T(8,128)(2,1)S(1)}, u32[]{:S(2)}, u32[]{:S(2)}) %collective-permute-start.1) | collective-permute-done | bytes 294944 | tf_op jit(solution)/shard_map/ppermute | solution.py:290
  14.4 7.3 %collective-permute-start.2 = (bf16[576,256]{1,0:T(8,128)(2,1)S(1)}, bf16[576,256]{1,0:T(8,128)(2,1)S(1)}, u32[]{:S(2)}, u32[]{:S(2)}) collective-permute-start(bf16[576,256]{1,0:T(8,128)(2,1)S(1)} %collective-permute-done.a_ref.b_ref), channel_id=1, source_target_pairs={{4,6},{5,7},{6,4},{7,5},{8,10},{9,11},{10,8},{11,9},{20,22},{21,23... | collective-permute-start | bytes 884744 | tf_op jit(solution)/shard_map/ppermute | solution.py:290
  22.0 0.1 select_reduce_fusion
  22.2 0.5 %collective-permute-start.5 = (bf16[576,256]{1,0:T(8,128)(2,1)S(1)}, bf16[576,256]{1,0:T(8,128)(2,1)S(1)}, u32[]{:S(2)}, u32[]{:S(2)}) collective-permute-start(bf16[576,256]{1,0:T(8,128)(2,1)S(1)} %shard_map.112.n0), channel_id=1, source_target_pairs={{0,1},{1,0},{2,3},{3,2},{4,5},{5,4},{6,7},{7,6},{8,9},{9,8},{10,11... | collective-permute-start | bytes 884744 | tf_op jit(solution)/shard_map/ppermute | solution.py:293
  22.7 6.9 %collective-permute-done.2.b_ref = bf16[576,256]{1,0:T(8,128)(2,1)S(1)} collective-permute-done((bf16[576,256]{1,0:T(8,128)(2,1)S(1)}, bf16[576,256]{1,0:T(8,128)(2,1)S(1)}, u32[]{:S(2)}, u32[]{:S(2)}) %collective-permute-start.2) | collective-permute-done | bytes 294944 | tf_op jit(solution)/shard_map/ppermute | solution.py:290
  29.7 5.4 %collective-permute-done.6.refs_2_ = bf16[576,256]{1,0:T(8,128)(2,1)S(1)} collective-permute-done((bf16[576,256]{1,0:T(8,128)(2,1)S(1)}, bf16[576,256]{1,0:T(8,128)(2,1)S(1)}, u32[]{:S(2)}, u32[]{:S(2)}) %collective-permute-start.6) | collective-permute-done | bytes 294944 | tf_op jit(solution)/shard_map/ppermute | solution.py:290
  35.2 1.6 %shard_map.113 = (f32[544,256]{1,0:T(8,128)S(1)}, f32[544,256]{1,0:T(8,128)S(1)}) custom-call(s32[4]{0:T(128)S(1)} %pad_add_fusion.1.ids_ref.refs_0_, bf16[4,544,576]{2,1,0:T(8,128)(2,1)S(1)} %shard_map.109.w_ref.refs_1_, bf16[576,256]{1,0:T(8,128)(2,1)S(1)} %shard_map.111.m0, bf16[576,256]{1,0:T(8,128)(2,1)S(1)} %collective-permute-done.4.m1, ...), custom_call_target="tpu_custom_call" | custom-call | flops 1000000000 | bytes 1048576 | tf_op jit(solution)/shard_map/pallas_call | solution.py:347
  36.8 1.4 %shard_map.115 = (f32[512,256]{1,0:T(8,128)S(1)}, bf16[512,256]{1,0:T(8,128)(2,1)S(1)}) custom-call(s32[4]{0:T(128)S(1)} %pad_add_fusion.1.ids_ref.refs_0_, bf16[4,544,576]{2,1,0:T(8,128)(2,1)S(1)} %shard_map.109.w_ref.refs_1_, bf16[576,256]{1,0:T(8,128)(2,1)S(1)} %collective-permute-done.6.refs_2_, bf16[576,256]{1,0:T(8,128)(2,1)S(1)} %collective-permute-done.7.refs_3_, ...), custom_call_target="tpu_custom_call" | custom-call | flops 500000000 | bytes 1048576 | tf_op jit(solution)/shard_map/pallas_call | solution.py:359
  38.3 1.4 %shard_map.114 = (f32[512,256]{1,0:T(8,128)S(1)}, bf16[256,256]{1,0:T(8,128)(2,1)S(1)}) custom-call(s32[4]{0:T(128)S(1)} %pad_add_fusion.1.ids_ref.refs_0_, bf16[4,544,576]{2,1,0:T(8,128)(2,1)S(1)} %shard_map.109.w_ref.refs_1_, bf16[576,256]{1,0:T(8,128)(2,1)S(1)} %shard_map.110.refs_2_, bf16[576,256]{1,0:T(8,128)(2,1)S(1)} %collective-permute-done.3.refs_3_, ...), custom_call_target="tpu_custom_call" | custom-call | flops 500000000 | bytes 1048576 | tf_op jit(solution)/shard_map/pallas_call | solution.py:364
  39.7 2.1 %collective-permute-start.9 = (bf16[256,256]{1,0:T(8,128)(2,1)S(1)}, bf16[256,256]{1,0:T(8,128)(2,1)S(1)}, u32[]{:S(2)}, u32[]{:S(2)}) collective-permute-start(bf16[256,256]{1,0:T(8,128)(2,1)S(1)} %get-tuple-element.31), channel_id=1, source_target_pairs={{0,8},{8,0},{1,9},{9,1},{2,10},{10,2},{3,11},{11,3},{4,12},{12,4},... | collective-permute-start | bytes 393224 | tf_op jit(solution)/shard_map/ppermute | solution.py:367
  41.7 0.5 %multiply_sine_fusion = (f32[64,512]{1,0:T(8,128)S(1)}, f32[64,512]{1,0:T(8,128)S(1)}) fusion(f32[512]{0:T(512)S(1)} %add_convert_fusion, f32[64]{0:T(128)S(1)} %multiply_exponential_fusion), kind=kLoop, calls=%fused_computation.1 | loop fusion | flops 32768 | bytes 264448 | tf_op jit(solution)/shard_map/sin | solution.py:308
  42.3 7.5 %collective-permute-done.9.refs_3_ = bf16[256,256]{1,0:T(8,128)(2,1)S(1)} collective-permute-done((bf16[256,256]{1,0:T(8,128)(2,1)S(1)}, bf16[256,256]{1,0:T(8,128)(2,1)S(1)}, u32[]{:S(2)}, u32[]{:S(2)}) %collective-permute-start.9) | collective-permute-done | bytes 131104 | tf_op jit(solution)/shard_map/ppermute | solution.py:367
  49.8 1.4 %shard_map.116 = bf16[256,256]{1,0:T(8,128)(2,1)} custom-call(f32[512,256]{1,0:T(8,128)S(1)} %get-tuple-element.27.refs_0_, bf16[512,256]{1,0:T(8,128)(2,1)S(1)} %collective-permute-done.8.refs_1_, f32[512,256]{1,0:T(8,128)S(1)} %get-tuple-element.30.refs_2_, bf16[256,256]{1,0:T(8,128)(2,1)S(1)} %collective-permute-done.9.refs_3_, ...), custom_call_target="tpu_custom_call" | custom-call | flops 1000000000 | bytes 1048576 | tf_op jit(solution)/shard_map/pallas_call | solution.py:374
  (33 shorter events, 0.6 us)
Async XLA Ops:
  0.0 13.9 %collective-permute-start = (bf16[576,256]{1,0:T(8,128)(2,1)}, bf16[576,256]{1,0:T(8,128)(2,1)S(1)}, u32[]{:S(2)}, u32[]{:S(2)}) collective-permute-start(bf16[576,256]{1,0:T(8,128)(2,1)} %bitcast.16), channel_id=1, source_target_pairs={{0,4},{1,5},{2,6},{3,7},{4,12},{5,13},{6,14},{7,15},{8,0},{9,1},{1... | collective-permute-start | bytes 884744 | tf_op jit(solution)/shard_map/ppermute | solution.py:290
  1.5 12.9 %collective-permute-start.1 = (bf16[576,256]{1,0:T(8,128)(2,1)}, bf16[576,256]{1,0:T(8,128)(2,1)S(1)}, u32[]{:S(2)}, u32[]{:S(2)}) collective-permute-start(bf16[576,256]{1,0:T(8,128)(2,1)} %bitcast.17), channel_id=1, source_target_pairs={{0,2},{1,3},{2,0},{3,1},{4,8},{5,9},{6,10},{7,11},{8,4},{9,5},{10,... | collective-permute-start | bytes 884744 | tf_op jit(solution)/shard_map/ppermute | solution.py:290
  9.5 1.3 %copy-start = (bf16[2304,256]{1,0:T(8,128)(2,1)S(1)}, bf16[2304,256]{1,0:T(8,128)(2,1)}, u32[]{:S(2)}) copy-start(bf16[2304,256]{1,0:T(8,128)(2,1)} %q_ref.1) | copy-start | bytes 3538948
  10.7 1.1 %copy-start.1 = (bf16[2304,128]{1,0:T(8,128)(2,1)S(1)}, bf16[2304,128]{1,0:T(8,128)(2,1)}, u32[]{:S(2)}) copy-start(bf16[2304,128]{1,0:T(8,128)(2,1)} %k_ref.1) | copy-start | bytes 1769476
  11.8 1.1 %copy-start.2 = (bf16[2304,128]{1,0:T(8,128)(2,1)S(1)}, bf16[2304,128]{1,0:T(8,128)(2,1)}, u32[]{:S(2)}) copy-start(bf16[2304,128]{1,0:T(8,128)(2,1)} %v_ref.1) | copy-start | bytes 1769476
  12.9 9.0 %copy-start.4 = (s32[12]{0:T(128)S(1)}, s32[12]{0:T(128)}, u32[]{:S(2)}) copy-start(s32[12]{0:T(128)} %param.20) | copy-start | bytes 148
  12.9 9.2 %copy-start.3 = (bf16[256,576]{0,1:T(8,128)(2,1)S(1)}, bf16[256,576]{0,1:T(8,128)(2,1)}, u32[]{:S(2)}) copy-start(bf16[256,576]{0,1:T(8,128)(2,1)} %param.11) | copy-start | bytes 884740
  14.4 15.2 %collective-permute-start.2 = (bf16[576,256]{1,0:T(8,128)(2,1)S(1)}, bf16[576,256]{1,0:T(8,128)(2,1)S(1)}, u32[]{:S(2)}, u32[]{:S(2)}) collective-permute-start(bf16[576,256]{1,0:T(8,128)(2,1)S(1)} %collective-permute-done.a_ref.b_ref), channel_id=1, source_target_pairs={{4,6},{5,7},{6,4},{7,5},{8,10},{9,11},{10,8},{11,9},{20,22},{21,23... | collective-permute-start | bytes 884744 | tf_op jit(solution)/shard_map/ppermute | solution.py:290
  21.8 13.4 %collective-permute-start.6 = (bf16[576,256]{1,0:T(8,128)(2,1)S(1)}, bf16[576,256]{1,0:T(8,128)(2,1)S(1)}, u32[]{:S(2)}, u32[]{:S(2)}) collective-permute-start(bf16[576,256]{1,0:T(8,128)(2,1)S(1)} %shard_map.111.m0), channel_id=1, source_target_pairs={{0,2},{1,3},{2,0},{3,1},{4,6},{5,7},{6,4},{7,5},{8,10},{9,11},{10,... | collective-permute-start | bytes 884744 | tf_op jit(solution)/shard_map/ppermute | solution.py:290
  22.1 13.1 %collective-permute-start.4 = (bf16[576,256]{1,0:T(8,128)(2,1)S(1)}, bf16[576,256]{1,0:T(8,128)(2,1)S(1)}, u32[]{:S(2)}, u32[]{:S(2)}) collective-permute-start(bf16[576,256]{1,0:T(8,128)(2,1)S(1)} %shard_map.111.m0), channel_id=1, source_target_pairs={{0,1},{1,0},{2,3},{3,2},{4,5},{5,4},{6,7},{7,6},{8,9},{9,8},{10,11... | collective-permute-start | bytes 884744 | tf_op jit(solution)/shard_map/ppermute | solution.py:293
  22.2 13.0 %collective-permute-start.5 = (bf16[576,256]{1,0:T(8,128)(2,1)S(1)}, bf16[576,256]{1,0:T(8,128)(2,1)S(1)}, u32[]{:S(2)}, u32[]{:S(2)}) collective-permute-start(bf16[576,256]{1,0:T(8,128)(2,1)S(1)} %shard_map.112.n0), channel_id=1, source_target_pairs={{0,1},{1,0},{2,3},{3,2},{4,5},{5,4},{6,7},{7,6},{8,9},{9,8},{10,11... | collective-permute-start | bytes 884744 | tf_op jit(solution)/shard_map/ppermute | solution.py:293
  29.6 8.6 %collective-permute-start.3 = (bf16[576,256]{1,0:T(8,128)(2,1)S(1)}, bf16[576,256]{1,0:T(8,128)(2,1)S(1)}, u32[]{:S(2)}, u32[]{:S(2)}) collective-permute-start(bf16[576,256]{1,0:T(8,128)(2,1)S(1)} %shard_map.110.refs_2_), channel_id=1, source_target_pairs={{0,1},{1,0},{2,3},{3,2},{4,5},{5,4},{6,7},{7,6},{8,9},{9,8},{10,11... | collective-permute-start | bytes 884744 | tf_op jit(solution)/shard_map/ppermute | solution.py:293
  35.2 1.6 %collective-permute-start.7 = (bf16[576,256]{1,0:T(8,128)(2,1)S(1)}, bf16[576,256]{1,0:T(8,128)(2,1)S(1)}, u32[]{:S(2)}, u32[]{:S(2)}) collective-permute-start(bf16[576,256]{1,0:T(8,128)(2,1)S(1)} %collective-permute-done.6.refs_2_), channel_id=1, source_target_pairs={{0,1},{1,0},{2,3},{3,2},{4,5},{5,4},{6,7},{7,6},{8,9},{9,8},{10,11... | collective-permute-start | bytes 884744 | tf_op jit(solution)/shard_map/ppermute | solution.py:293
  38.2 11.6 %collective-permute-start.8 = (bf16[512,256]{1,0:T(8,128)(2,1)S(1)}, bf16[512,256]{1,0:T(8,128)(2,1)S(1)}, u32[]{:S(2)}, u32[]{:S(2)}) collective-permute-start(bf16[512,256]{1,0:T(8,128)(2,1)S(1)} %get-tuple-element.29), channel_id=1, source_target_pairs={{0,8},{8,0},{1,9},{9,1},{2,10},{10,2},{3,11},{11,3},{4,12},{12,4},... | collective-permute-start | bytes 786440 | tf_op jit(solution)/shard_map/ppermute | solution.py:363
  39.7 10.1 %collective-permute-start.9 = (bf16[256,256]{1,0:T(8,128)(2,1)S(1)}, bf16[256,256]{1,0:T(8,128)(2,1)S(1)}, u32[]{:S(2)}, u32[]{:S(2)}) collective-permute-start(bf16[256,256]{1,0:T(8,128)(2,1)S(1)} %get-tuple-element.31), channel_id=1, source_target_pairs={{0,8},{8,0},{1,9},{9,1},{2,10},{10,2},{3,11},{11,3},{4,12},{12,4},... | collective-permute-start | bytes 393224 | tf_op jit(solution)/shard_map/ppermute | solution.py:367

commit v3 on v0

--- a/solution.py
+++ b/solution.py
@@ -3,7 +3,10 @@
 import jax
 import jax.numpy as jnp
 from jax import lax
+from jax.experimental import pallas as pl
+from jax.experimental.pallas import tpu as pltpu
 from jax.sharding import PartitionSpec as P
+
 
 HD = 128
 
@@ -137,6 +140,347 @@
     return attended.reshape(tok_rows, local_heads * HD).astype(jnp.bfloat16)
 
 
+VMEM = pl.BlockSpec(memory_space=pltpu.VMEM)
+SMEM = pl.BlockSpec(memory_space=pltpu.SMEM)
+HBM = pl.BlockSpec(memory_space=pltpu.HBM)
+F32, BF16 = jnp.float32, jnp.bfloat16
+
+
+def in_hbm(x):
+    return pltpu.with_memory_space_constraint(x, pltpu.HBM)
+
+
+def call(body, outs, in_specs, flops, **kw):
+    multi = isinstance(outs, (list, tuple))
+    return pl.pallas_call(
+        body,
+        out_shape=outs,
+        in_specs=in_specs,
+        out_specs=[VMEM] * len(outs) if multi else VMEM,
+        cost_estimate=pl.CostEstimate(flops=flops, bytes_accessed=1 << 20, transcendentals=0),
+        compiler_params=pltpu.CompilerParams(vmem_limit_bytes=12 << 20),
+        **kw,
+    )
+
+
+def place_of():
+    c, h = lax.axis_index("ctx"), lax.axis_index("head")
+    z = lax.shift_right_logical(h, 1)
+    k = lax.bitwise_and(h, 1)
+    near = lax.shift_right_logical(z, 1) == c
+    return c, z, k, near
+
+
+def rows_of(second):
+    _, z, k, _ = place_of()
+    base = lax.bitwise_and(z, 1) * 2
+    if second:
+        base = 2 - base
+    return base + k, base + 1 - k
+
+
+def dot(a, b):
+    return jnp.dot(a, b, preferred_element_type=F32)
+
+
+def setup_body(
+    block_len, order_ref, starts_ref, prompt_ref, q_hbm, k_hbm, v_hbm, dq_hbm, dv_hbm,
+    w_out, vis_out, pos_out, q_ref, k_ref, v_ref, dq_ref, dv_ref, sems,
+):
+    c, _, _, _ = place_of()
+    half = q_ref.shape[0]
+    here = pl.ds(pl.multiple_of(c * half, 128), half)
+    copies = [
+        pltpu.make_async_copy(src, dst, sems.at[i])
+        for i, (src, dst) in enumerate(
+            [
+                (q_hbm, q_ref),
+                (k_hbm, k_ref),
+                (v_hbm, v_ref),
+                (dq_hbm.at[:, here], dq_ref),
+                (dv_hbm.at[:, here], dv_ref),
+            ]
+        )
+    ]
+    for copy in copies:
+        copy.start()
+
+    keys, rows = vis_out.shape
+    lane = lax.broadcasted_iota(jnp.int32, (8, keys), 1)
+    row = jnp.where(lane < rows, lane + c * rows, lane - c * rows)
+    block = jnp.zeros_like(row)
+    for i in range(1, order_ref.shape[0]):
+        block += (row >= i * block_len).astype(jnp.int32)
+    inside = row - block * block_len
+    place = inside
+    for i in range(order_ref.shape[0]):
+        place = jnp.where(block == i, order_ref[i] * block_len + inside, place)
+    segs = starts_ref.shape[0]
+    segment, begin, prompt = jnp.zeros_like(row), jnp.zeros_like(row), jnp.zeros_like(row)
+    for j in range(segs):
+        reached = starts_ref[j] <= place
+        segment = jnp.where(reached, j, segment)
+        begin = jnp.where(reached, starts_ref[j], begin)
+        prompt = jnp.where(reached, prompt_ref[j], prompt)
+    length = jnp.zeros_like(row)
+    for j in range(segs):
+        end = starts_ref[j + 1] if j + 1 < segs else keys
+        length = jnp.where(prompt == j, end - starts_ref[j], length)
+    moved = place - begin + jnp.where(prompt != segment, length, 0)
+    pos_out[...] = moved.astype(F32)
+    key_seg = segment.astype(F32).T[:, :1]
+    key_place = place.astype(F32).T[:, :1]
+    mine = lambda x: x[:1, :rows].astype(F32)
+    q_seg, q_place, q_prompt = mine(segment), mine(place), mine(prompt)
+    q_from = jnp.where(q_prompt != q_seg, q_prompt, -1.0)
+    same = (key_seg == q_seg) & (key_place <= q_place)
+    vis_out[...] = jnp.where(same | (key_seg == q_from), 1.0, 0.0)
+
+    for copy in copies:
+        copy.wait()
+    depth = w_out.shape[2]
+    for b in range(w_out.shape[0]):
+        at = 0
+        span = slice(b * depth, (b + 1) * depth)
+        for ref in (q_ref, k_ref, v_ref):
+            w_out[b, at : at + ref.shape[1], :] = ref[span, :].T
+            at += ref.shape[1]
+        for ref in (dq_ref, dv_ref):
+            w_out[b, at : at + ref.shape[0], :] = ref[:, span]
+            at += ref.shape[0]
+
+
+def first_body(w_ref, m0, m1, n0, n1, out_m, out_n):
+    own, twin = rows_of(False)
+    out_m[...] = dot(w_ref[own], m0[...]) + dot(w_ref[twin], m1[...])
+    out_n[...] = dot(w_ref[own], n0[...]) + dot(w_ref[twin], n1[...])
+
+
+def second_body(wide_q, first_sent, w_ref, x0, x1, part, eq_ref, ev_ref, keep, send):
+    own, twin = rows_of(True)
+    total = part[...] + dot(w_ref[own], x0[...]) + dot(w_ref[twin], x1[...])
+    rank, wide_v = ev_ref.shape
+    wide = send.shape[0] + first_sent
+    low_q = (adapter_scaling * total[wide : wide + rank].astype(BF16)).astype(BF16)
+    low_v = (adapter_scaling * total[wide + rank : wide + 2 * rank].astype(BF16)).astype(BF16)
+    over = (((0,), (0,)), ((), ()))
+    grow = lambda e, low: lax.dot_general(e[...], low, over, preferred_element_type=F32)
+    query = total[:wide_q] + grow(eq_ref, low_q)
+    key = total[wide_q : wide - wide_v]
+    value = total[wide - wide_v : wide] + grow(ev_ref, low_v)
+    keep[:wide_q] = query
+    keep[wide_q : wide - wide_v] = key
+    keep[wide - wide_v :] = value
+    if first_sent == 0:
+        send[:wide_q] = query.astype(BF16)
+    send[wide_q - first_sent : wide - wide_v - first_sent] = key.astype(BF16)
+    send[wide - wide_v - first_sent :] = value.astype(BF16)
+
+
+def pick_body(a_ref, b_ref, out_ref):
+    near = place_of()[3]
+
+    @pl.when(near)
+    def _():
+        out_ref[...] = a_ref[...]
+
+    @pl.when(jnp.logical_not(near))
+    def _():
+        out_ref[...] = b_ref[...]
+
+
+def turn(x, cos, sin):
+    half = x.shape[0] // 2
+    a, b = x[:half], x[half:]
+    return jnp.concatenate([a * cos - b * sin, b * cos + a * sin], axis=0)
+
+
+def weigh(keys, queries, values, visible, heads):
+    rows = visible.shape[1]
+    scores = dot(keys.T, queries)
+    weights = jnp.exp(softcap_limit * jnp.tanh(scores / softcap_limit))
+    sums, products = [], []
+    for h in range(heads):
+        w = weights[:, h * rows : (h + 1) * rows] * visible
+        sums.append(jnp.sum(w, axis=0, keepdims=True))
+        products.append(dot(values, w.astype(BF16)))
+    return jnp.concatenate(sums, axis=1), jnp.concatenate(products, axis=1)
+
+
+def near_body(heads, mine, mine_in, cos_ref, sin_ref, vis_ref, q_out, sum_out, num_out):
+    rows = mine.shape[1]
+    wide_q = heads * HD
+    cos, sin = cos_ref[:, :rows], sin_ref[:, :rows]
+    total = mine[...] + mine_in[...].astype(F32)
+    queries = jnp.concatenate(
+        [
+            (turn(total[h * HD : (h + 1) * HD], cos, sin) * query_scale).astype(BF16)
+            for h in range(heads)
+        ],
+        axis=1,
+    )
+    keys = turn(total[wide_q : wide_q + HD], cos, sin).astype(BF16)
+    values = total[wide_q + HD :].astype(BF16)
+    q_out[...] = queries
+    sums, num_out[...] = weigh(keys, queries, values, vis_ref[:rows, :], heads)
+    sum_out[...] = jnp.broadcast_to(sums, sum_out.shape)
+
+
+def far_body(heads, other, other_in, q_ref, sum_ref, num_ref, cos_ref, sin_ref, vis_ref, out_ref):
+    rows = other.shape[1]
+    rest = other[heads * HD :] + other_in[...].astype(F32)
+    keys = turn(rest[:HD], cos_ref[:, rows:], sin_ref[:, rows:]).astype(BF16)
+    sums, products = weigh(
+        keys, q_ref[...], rest[HD:].astype(BF16), vis_ref[rows:, :], heads
+    )
+    done = (num_ref[...] + products) / (sum_ref[:1, :] + sums)
+    for h in range(heads):
+        out_ref[:, h * HD : (h + 1) * HD] = done[:, h * rows : (h + 1) * rows].T.astype(BF16)
+
+
+def local_fast(
+    tokens,
+    query_frozen_matrix,
+    key_weight,
+    value_frozen_matrix,
+    query_down,
+    query_adapter_expand,
+    value_down,
+    value_adapter_expand,
+    block_order,
+    doc_starts,
+    prompt_of,
+):
+    rows, depth = tokens.shape
+    chips = lax.axis_size("head") // 2
+    both = ("ctx", "head")
+
+    def at(ci, zi, ki):
+        return ci * chips * 2 + zi * 2 + ki
+
+    q1_pairs, q2_pairs, z_pairs, zf_pairs = [], [], [], []
+    for ci in range(2):
+        for zi in range(chips):
+            for ki in range(2):
+                me = at(ci, zi, ki)
+                z_pairs.append((me, at(ci, zi ^ 1, ki)))
+                if zi // 2 == ci:
+                    q1_pairs.append((me, at(ci, zi ^ 2, ki)))
+                    q2_pairs.append((me, at(ci, zi ^ 1, ki)))
+                else:
+                    q1_pairs.append((me, at(1 - ci, zi, ki)))
+                    q2_pairs.append((me, at(1 - ci, zi ^ 2, ki)))
+                    zf_pairs.append((me, at(ci, zi ^ 1, ki)))
+    core = [(i, i ^ 1) for i in range(chips * 2)]
+    swap = [(0, 1), (1, 0)]
+
+    def send(x, pairs, axes=both):
+        return lax.ppermute(x, axes, pairs)
+
+    def twin(x):
+        return send(x, core, "head")
+
+    own = tokens.T
+    q1 = send(own, q1_pairs)
+    q2 = send(own, q2_pairs)
+
+    wide_q, wide_kv = query_frozen_matrix.shape[1], key_weight.shape[1]
+    wide = wide_q + 2 * wide_kv
+    rank = query_down.shape[1]
+    half = query_frozen_matrix.shape[0]
+    keys = 2 * rows
+
+    def setup(*refs):
+        setup_body(rows // 2, *refs)
+
+    weights, visible, moved = pl.pallas_call(
+        setup,
+        out_shape=[
+            jax.ShapeDtypeStruct((half // depth, wide + 2 * rank, depth), BF16),
+            jax.ShapeDtypeStruct((keys, rows), F32),
+            jax.ShapeDtypeStruct((8, keys), F32),
+        ],
+        in_specs=[SMEM] * 3 + [HBM] * 5,
+        out_specs=[VMEM] * 3,
+        scratch_shapes=[
+            pltpu.VMEM((half, wide_q), BF16),
+            pltpu.VMEM((half, wide_kv), BF16),
+            pltpu.VMEM((half, wide_kv), BF16),
+            pltpu.VMEM((rank, half), BF16),
+            pltpu.VMEM((rank, half), BF16),
+            pltpu.SemaphoreType.DMA((5,)),
+        ],
+        cost_estimate=pl.CostEstimate(flops=10**9, bytes_accessed=1 << 20, transcendentals=0),
+        compiler_params=pltpu.CompilerParams(vmem_limit_bytes=12 << 20),
+    )(
+        block_order,
+        doc_starts,
+        prompt_of,
+        in_hbm(query_frozen_matrix),
+        in_hbm(key_weight),
+        in_hbm(value_frozen_matrix),
+        in_hbm(query_down.T),
+        in_hbm(value_down.T),
+    )
+
+    def pick(a, b):
+        out = jax.ShapeDtypeStruct(a.shape, a.dtype)
+        return call(pick_body, out, [VMEM, VMEM], 10**7)(a, b)
+
+    other_a = pick(q1, q2)
+    other_b = send(other_a, z_pairs)
+    late = send(q1, zf_pairs)
+    mine_a = pick(own, q1)
+    mine_b = pick(q2, late)
+
+    whole = jax.ShapeDtypeStruct((wide + 2 * rank, rows), F32)
+    kept = jax.ShapeDtypeStruct((wide, rows), F32)
+    other_twin, mine_twin = twin(other_a), twin(mine_a)
+    part_m, part_n = call(first_body, [whole, whole], [VMEM] * 5, 10**9)(
+        weights, other_a, other_twin, mine_a, mine_twin
+    )
+
+    def second(x, part, first_sent):
+        def body(*refs):
+            second_body(wide_q, first_sent, *refs)
+
+        outs = [kept, jax.ShapeDtypeStruct((wide - first_sent, rows), BF16)]
+        other = twin(x)
+        return call(body, outs, [VMEM] * 6, 5 * 10**8)(
+            weights, x, other, part, query_adapter_expand, value_adapter_expand
+        )
+
+    other_keep, other_send = second(other_b, part_m, 0)
+    mine_in = send(other_send, swap, "ctx")
+    frequency = jnp.exp(
+        jnp.arange(HD // 2, dtype=F32) * (-2.0 * math.log(rope_base) / HD)
+    )
+    angles = frequency[:, None] * moved[:1]
+    cos, sin = jnp.cos(angles), jnp.sin(angles)
+    mine_keep, mine_send = second(mine_b, part_n, wide_q)
+    other_in = send(mine_send, swap, "ctx")
+
+    heads = wide_q // HD
+
+    def near_keys(*refs):
+        near_body(heads, *refs)
+
+    def far_keys(*refs):
+        far_body(heads, *refs)
+
+    outs = [
+        jax.ShapeDtypeStruct((HD, heads * rows), BF16),
+        jax.ShapeDtypeStruct((8, heads * rows), F32),
+        jax.ShapeDtypeStruct((HD, heads * rows), F32),
+    ]
+    queries, sums, products = call(near_keys, outs, [VMEM] * 5, 10**9)(
+        mine_keep, mine_in, cos, sin, visible
+    )
+    return call(far_keys, jax.ShapeDtypeStruct((rows, wide_q), BF16), [VMEM] * 8, 10**9)(
+        other_keep, other_in, queries, sums, products, cos, sin, visible
+    )
+
+
 def solution(mesh):
     in_specs = (
         P(("tenant", "ctx"), "head"),
@@ -152,4 +496,13 @@
         P("tenant"),
     )
     out_specs = P(("tenant", "ctx"), "head")
-    return jax.shard_map(local, mesh=mesh, in_specs=in_specs, out_specs=out_specs, check_vma=False)
+    fits = mesh.shape["ctx"] == 2 and mesh.shape["head"] == 8
+
+    def body(*args):
+        if not fits:
+            return local(*args)
+        return local_fast(*args)
+
+    return jax.shard_map(
+        body, mesh=mesh, in_specs=in_specs, out_specs=out_specs, check_vma=False
+    )

time: 144 us -> 53.6 us (0.37)
  waiting for transfers between devices: 105 us -> 28.5 us
  between operations: 13.3 us -> 0.17 us
  starting transfers between devices: 0.15 us -> 13.1 us
  matrix products: 11.6 us -> 0 us
  blocking collectives: 9.87 us -> 0 us
  Pallas kernels: 0 us -> 7.59 us
  local copies, waits for them, and re-layouts: 0.86 us -> 2.94 us
    all_gather x4 -> x0, waiting for transfers between devices: 102 us -> none  [the longest x1 32.4 us: local(): full_tokens = lax.all_gather(tokens, 'head', axis=1, tiled=True)]
    ppermute x0 -> x10, waiting for transfers between devices: none -> 28.5 us  [send(): return lax.ppermute(x, axes, pairs)]
    ppermute x0 -> x10, starting transfers between devices: none -> 13.1 us  [send(): return lax.ppermute(x, axes, pairs)]
    dot_general x7 -> x0, matrix products: 11.6 us -> none  [the longest x3 7.33 us: add_rows(): return jnp.dot(full_tokens, weight_part, preferred_element_type=jnp.float32)]
    all_gather x2 -> x0, blocking collectives: 9.87 us -> none  [the longest x1 4.93 us: local(): lax.all_gather(key_proj, 'ctx', axis=0, tiled=True)]
    pallas_call x0 -> x9, Pallas kernels: none -> 7.59 us  [the longest x1 3.02 us: local_fast(): pl.pallas_call(setup, out_shape=[jax.ShapeDtypeStruct((half // depth, wid...]
    unnamed x12, local copies, waits for them, and re-layouts: 0.03 us -> 2.94 us
    unnamed x4 -> x0, waiting for transfers between devices: 2.58 us -> none
  transfers between devices with their start and end apart: 4 -> 10, of which waited for: 4 -> 5; matrix products, arithmetic and copies ran while one was open for 7% -> 1% of each run, Pallas kernels for 0% -> 12%
where the time goes in v3:
time: 53.6 us; the launch traced here: 52.9 us
  waiting for transfers between devices  28.5 us (53%)
  starting transfers between devices  13.1 us (24%)
  Pallas kernels  7.59 us (14%)
  local copies, waits for them, and re-layouts  2.94 us (5%)
  other arithmetic  0.54 us (1%)
    ppermute x10, waiting for transfers between devices, send(): return lax.ppermute(x, axes, pairs)  28.5 us
    ppermute x10, starting transfers between devices, send(): return lax.ppermute(x, axes, pairs)  13.1 us
    pallas_call x1, Pallas kernels, local_fast(): pl.pallas_call(setup, out_shape=[jax.ShapeDtypeStruct((half // depth, wid...  3.02 us
    unnamed x12, local copies, waits for them, and re-layouts  2.94 us
    pallas_call x2, Pallas kernels, second(): call(body, outs, [VMEM] * 6, 5 * 10 ** 8)  1.69 us
    pallas_call x1, Pallas kernels, local_fast(): call(far_keys, jax.ShapeDtypeStruct((rows, wide_q), BF16), [VMEM] * 8, 10...  1.23 us
  transfers between devices with their start and end apart: 10, of which 5 were waited for; matrix products, arithmetic and copies ran while one was open for 1% of the time, Pallas kernels for 12%

profile of v3, /device:TPU:16, one launch (start us, length us, event | category | flops | bytes accessed | tf_op | source)
XLA Modules:
  0.0 52.9 jit_solution(2083156766096787875)
XLA Ops:
  0.0 1.5 %collective-permute-start = (bf16[576,256]{1,0:T(8,128)(2,1)}, bf16[576,256]{1,0:T(8,128)(2,1)S(1)}, u32[]{:S(2)}, u32[]{:S(2)}) collective-permute-start(bf16[576,256]{1,0:T(8,128)(2,1)} %bitcast.4), channel_id=1, source_target_pairs={{0,4},{1,5},{2,6},{3,7},{4,12},{5,13},{6,14},{7,15},{8,0},{9,1},{1... | collective-permute-start | bytes 884744 | tf_op jit(solution)/shard_map/ppermute | solution.py:378
  1.5 0.0 collective-permute-start.1
  1.5 9.5 %collective-permute-done.a_ref.b_ref = bf16[576,256]{1,0:T(8,128)(2,1)S(1)} collective-permute-done((bf16[576,256]{1,0:T(8,128)(2,1)}, bf16[576,256]{1,0:T(8,128)(2,1)S(1)}, u32[]{:S(2)}, u32[]{:S(2)}) %collective-permute-start) | collective-permute-done | bytes 294944 | tf_op jit(solution)/shard_map/ppermute | solution.py:378
  11.0 8.5 %collective-permute-start.6 = (bf16[576,256]{1,0:T(8,128)(2,1)S(1)}, bf16[576,256]{1,0:T(8,128)(2,1)S(1)}, u32[]{:S(2)}, u32[]{:S(2)}) collective-permute-start(bf16[576,256]{1,0:T(8,128)(2,1)S(1)} %collective-permute-done.a_ref.b_ref), channel_id=1, source_target_pairs={{4,6},{5,7},{6,4},{7,5},{8,10},{9,11},{10,8},{11,9},{20,22},{21,23... | collective-permute-start | bytes 884744 | tf_op jit(solution)/shard_map/ppermute | solution.py:378
  19.5 0.0 collective-permute-done.1.b_ref.a_ref
  19.6 0.3 collective-permute-start.2
  19.9 0.0 collective-permute-start.4
  19.9 1.0 %copy-done = bf16[256,576]{0,1:T(8,128)(2,1)S(1)} copy-done((bf16[256,576]{0,1:T(8,128)(2,1)S(1)}, bf16[256,576]{0,1:T(8,128)(2,1)}, u32[]{:S(2)}) %copy-start) | copy-done | bytes 294936
  20.9 0.6 %collective-permute-start.5 = (bf16[576,256]{1,0:T(8,128)(2,1)S(1)}, bf16[576,256]{1,0:T(8,128)(2,1)S(1)}, u32[]{:S(2)}, u32[]{:S(2)}) collective-permute-start(bf16[576,256]{1,0:T(8,128)(2,1)S(1)} %shard_map.111.n0), channel_id=1, source_target_pairs={{0,1},{1,0},{2,3},{3,2},{4,5},{5,4},{6,7},{7,6},{8,9},{9,8},{10,11... | collective-permute-start | bytes 884744 | tf_op jit(solution)/shard_map/ppermute | solution.py:378
  21.5 5.9 %collective-permute-done.6.b_ref = bf16[576,256]{1,0:T(8,128)(2,1)S(1)} collective-permute-done((bf16[576,256]{1,0:T(8,128)(2,1)S(1)}, bf16[576,256]{1,0:T(8,128)(2,1)S(1)}, u32[]{:S(2)}, u32[]{:S(2)}) %collective-permute-start.6) | collective-permute-done | bytes 294944 | tf_op jit(solution)/shard_map/ppermute | solution.py:378
  27.4 0.1 collective-permute-start.7
  27.5 5.5 %collective-permute-done.2.refs_1_ = bf16[576,256]{1,0:T(8,128)(2,1)S(1)} collective-permute-done((bf16[576,256]{1,0:T(8,128)(2,1)S(1)}, bf16[576,256]{1,0:T(8,128)(2,1)S(1)}, u32[]{:S(2)}, u32[]{:S(2)}) %collective-permute-start.2) | collective-permute-done | bytes 294944 | tf_op jit(solution)/shard_map/ppermute | solution.py:378
  33.0 0.0 collective-permute-start.3
  33.0 0.7 %copy-done.3 = s32[4]{0:T(128)S(1)} copy-done((s32[4]{0:T(128)S(1)}, s32[4]{0:T(128)}, u32[]{:S(2)}) %copy-start.3) | copy-done | bytes 40
  33.7 0.7 %copy-done.4 = s32[12]{0:T(128)S(1)} copy-done((s32[12]{0:T(128)S(1)}, s32[12]{0:T(128)}, u32[]{:S(2)}) %copy-start.4) | copy-done | bytes 72
  34.4 0.7 %copy-done.5 = s32[12]{0:T(128)S(1)} copy-done((s32[12]{0:T(128)S(1)}, s32[12]{0:T(128)}, u32[]{:S(2)}) %copy-start.5) | copy-done | bytes 72
  35.0 3.0 %shard_map.109 = (bf16[4,544,576]{2,1,0:T(8,128)(2,1)S(1)}, f32[512,256]{1,0:T(8,128)S(1)}, f32[8,512]{1,0:T(8,128)S(1)}) custom-call(s32[4]{0:T(128)S(1)} %copy-done.3, s32[12]{0:T(128)S(1)} %copy-done.4, s32[12]{0:T(128)S(1)} %copy-done.5, bf16[2304,256]{1,0:T(8,128)(2,1)} %refs_3_.1, bf16[2304,128]{1,0:T(8,128)(2,1)} %refs_4_.3, ...), custom_call_target="tpu_custom_call" | custom-call | flops 1000000000 | bytes 1048576 | tf_op jit(solution)/shard_map/pallas_call | solution.py:396
  38.0 0.0 copy-start.1
  38.0 0.0 copy-start.2
  38.1 0.0 collective-permute-done.4.m1
  38.1 0.0 collective-permute-done.5.n1
  38.1 1.0 %shard_map.112 = (f32[544,256]{1,0:T(8,128)S(1)}, f32[544,256]{1,0:T(8,128)S(1)}) custom-call(bf16[4,544,576]{2,1,0:T(8,128)(2,1)S(1)} %get-tuple-element.17.w_ref.refs_0_, bf16[576,256]{1,0:T(8,128)(2,1)S(1)} %shard_map.110.m0, bf16[576,256]{1,0:T(8,128)(2,1)S(1)} %collective-permute-done.4.m1, bf16[576,256]{1,0:T(8,128)(2,1)S(1)} %shard_map.111.n0, ...), custom_call_target="tpu_custom_call" | custom-call | flops 1000000000 | bytes 1048576 | tf_op jit(solution)/shard_map/pallas_call | solution.py:439
  39.2 0.0 collective-permute-done.3.refs_2_
  39.2 0.8 %shard_map.113 = (f32[512,256]{1,0:T(8,128)S(1)}, bf16[512,256]{1,0:T(8,128)(2,1)S(1)}) custom-call(bf16[4,544,576]{2,1,0:T(8,128)(2,1)S(1)} %get-tuple-element.17.w_ref.refs_0_, bf16[576,256]{1,0:T(8,128)(2,1)S(1)} %collective-permute-done.2.refs_1_, bf16[576,256]{1,0:T(8,128)(2,1)S(1)} %collective-permute-done.3.refs_2_, ...), custom_call_target="tpu_custom_call" | custom-call | flops 500000000 | bytes 1048576 | tf_op jit(solution)/shard_map/pallas_call | solution.py:449
  40.0 0.1 collective-permute-start.9
  40.1 0.8 %shard_map.115 = (f32[512,256]{1,0:T(8,128)S(1)}, bf16[256,256]{1,0:T(8,128)(2,1)S(1)}) custom-call(bf16[4,544,576]{2,1,0:T(8,128)(2,1)S(1)} %get-tuple-element.17.w_ref.refs_0_, bf16[576,256]{1,0:T(8,128)(2,1)S(1)} %shard_map.114.refs_1_, bf16[576,256]{1,0:T(8,128)(2,1)S(1)} %collective-permute-done.7.refs_2_, f32[544,256]{1,0:T(8,128)S(1)} %get-tuple-element.20.refs_3_, ...), custom_call_target="tpu_custom_call" | custom-call | flops 500000000 | bytes 1048576 | tf_op jit(solution)/shard_map/pallas_call | solution.py:449
  41.0 2.1 %collective-permute-start.8 = (bf16[256,256]{1,0:T(8,128)(2,1)S(1)}, bf16[256,256]{1,0:T(8,128)(2,1)S(1)}, u32[]{:S(2)}, u32[]{:S(2)}) collective-permute-start(bf16[256,256]{1,0:T(8,128)(2,1)S(1)} %get-tuple-element.21), channel_id=1, source_target_pairs={{0,8},{8,0},{1,9},{9,1},{2,10},{10,2},{3,11},{11,3},{4,12},{12,4},... | collective-permute-start | bytes 393224 | tf_op jit(solution)/shard_map/ppermute | solution.py:378
  43.1 0.5 %multiply_sine_fusion = (f32[64,512]{1,0:T(8,128)S(1)}, f32[64,512]{1,0:T(8,128)S(1)}) fusion(f32[512]{0:T(512)S(1)} %bitcast.7, f32[64]{0:T(128)S(1)} %multiply_exponential_fusion), kind=kLoop, calls=%fused_computation | loop fusion | flops 32768 | bytes 264448 | tf_op jit(solution)/shard_map/sin | solution.py:459
  43.6 5.7 %collective-permute-done.9.refs_1_ = bf16[512,256]{1,0:T(8,128)(2,1)S(1)} collective-permute-done((bf16[512,256]{1,0:T(8,128)(2,1)S(1)}, bf16[512,256]{1,0:T(8,128)(2,1)S(1)}, u32[]{:S(2)}, u32[]{:S(2)}) %collective-permute-start.9) | collective-permute-done | bytes 262176 | tf_op jit(solution)/shard_map/ppermute | solution.py:378
  49.3 0.5 shard_map.116
  49.8 1.8 %collective-permute-done.8.refs_1_ = bf16[256,256]{1,0:T(8,128)(2,1)S(1)} collective-permute-done((bf16[256,256]{1,0:T(8,128)(2,1)S(1)}, bf16[256,256]{1,0:T(8,128)(2,1)S(1)}, u32[]{:S(2)}, u32[]{:S(2)}) %collective-permute-start.8) | collective-permute-done | bytes 131104 | tf_op jit(solution)/shard_map/ppermute | solution.py:378
  51.6 1.2 %shard_map.117 = bf16[256,256]{1,0:T(8,128)(2,1)} custom-call(f32[512,256]{1,0:T(8,128)S(1)} %get-tuple-element.19.refs_0_, bf16[256,256]{1,0:T(8,128)(2,1)S(1)} %collective-permute-done.8.refs_1_, bf16[128,512]{1,0:T(8,128)(2,1)S(1)} %get-tuple-element.26.refs_2_, f32[8,512]{1,0:T(8,128)S(1)} %get-tuple-element.27.refs_3_, ...), custom_call_target="tpu_custom_call" | custom-call | flops 1000000000 | bytes 1048576 | tf_op jit(solution)/shard_map/pallas_call | solution.py:479
  (12 shorter events, 0.1 us)
Async XLA Ops:
  0.0 11.0 %collective-permute-start = (bf16[576,256]{1,0:T(8,128)(2,1)}, bf16[576,256]{1,0:T(8,128)(2,1)S(1)}, u32[]{:S(2)}, u32[]{:S(2)}) collective-permute-start(bf16[576,256]{1,0:T(8,128)(2,1)} %bitcast.4), channel_id=1, source_target_pairs={{0,4},{1,5},{2,6},{3,7},{4,12},{5,13},{6,14},{7,15},{8,0},{9,1},{1... | collective-permute-start | bytes 884744 | tf_op jit(solution)/shard_map/ppermute | solution.py:378
  1.5 18.1 %collective-permute-start.1 = (bf16[576,256]{1,0:T(8,128)(2,1)}, bf16[576,256]{1,0:T(8,128)(2,1)S(1)}, u32[]{:S(2)}, u32[]{:S(2)}) collective-permute-start(bf16[576,256]{1,0:T(8,128)(2,1)} %bitcast.5), channel_id=1, source_target_pairs={{0,2},{1,3},{2,0},{3,1},{4,8},{5,9},{6,10},{7,11},{8,4},{9,5},{10,... | collective-permute-start | bytes 884744 | tf_op jit(solution)/shard_map/ppermute | solution.py:378
  11.0 16.4 %collective-permute-start.6 = (bf16[576,256]{1,0:T(8,128)(2,1)S(1)}, bf16[576,256]{1,0:T(8,128)(2,1)S(1)}, u32[]{:S(2)}, u32[]{:S(2)}) collective-permute-start(bf16[576,256]{1,0:T(8,128)(2,1)S(1)} %collective-permute-done.a_ref.b_ref), channel_id=1, source_target_pairs={{4,6},{5,7},{6,4},{7,5},{8,10},{9,11},{10,8},{11,9},{20,22},{21,23... | collective-permute-start | bytes 884744 | tf_op jit(solution)/shard_map/ppermute | solution.py:378
  19.6 13.4 %collective-permute-start.2 = (bf16[576,256]{1,0:T(8,128)(2,1)S(1)}, bf16[576,256]{1,0:T(8,128)(2,1)S(1)}, u32[]{:S(2)}, u32[]{:S(2)}) collective-permute-start(bf16[576,256]{1,0:T(8,128)(2,1)S(1)} %shard_map.110.m0), channel_id=1, source_target_pairs={{0,2},{1,3},{2,0},{3,1},{4,6},{5,7},{6,4},{7,5},{8,10},{9,11},{10,... | collective-permute-start | bytes 884744 | tf_op jit(solution)/shard_map/ppermute | solution.py:378
  19.9 18.1 %collective-permute-start.4 = (bf16[576,256]{1,0:T(8,128)(2,1)S(1)}, bf16[576,256]{1,0:T(8,128)(2,1)S(1)}, u32[]{:S(2)}, u32[]{:S(2)}) collective-permute-start(bf16[576,256]{1,0:T(8,128)(2,1)S(1)} %shard_map.110.m0), channel_id=1, source_target_pairs={{0,1},{1,0},{2,3},{3,2},{4,5},{5,4},{6,7},{7,6},{8,9},{9,8},{10,11... | collective-permute-start | bytes 884744 | tf_op jit(solution)/shard_map/ppermute | solution.py:378
  19.9 1.0 %copy-start = (bf16[256,576]{0,1:T(8,128)(2,1)S(1)}, bf16[256,576]{0,1:T(8,128)(2,1)}, u32[]{:S(2)}) copy-start(bf16[256,576]{0,1:T(8,128)(2,1)} %param.11) | copy-start | bytes 884740
  20.9 17.2 %collective-permute-start.5 = (bf16[576,256]{1,0:T(8,128)(2,1)S(1)}, bf16[576,256]{1,0:T(8,128)(2,1)S(1)}, u32[]{:S(2)}, u32[]{:S(2)}) collective-permute-start(bf16[576,256]{1,0:T(8,128)(2,1)S(1)} %shard_map.111.n0), channel_id=1, source_target_pairs={{0,1},{1,0},{2,3},{3,2},{4,5},{5,4},{6,7},{7,6},{8,9},{9,8},{10,11... | collective-permute-start | bytes 884744 | tf_op jit(solution)/shard_map/ppermute | solution.py:378
  27.4 12.7 %collective-permute-start.7 = (bf16[576,256]{1,0:T(8,128)(2,1)S(1)}, bf16[576,256]{1,0:T(8,128)(2,1)S(1)}, u32[]{:S(2)}, u32[]{:S(2)}) collective-permute-start(bf16[576,256]{1,0:T(8,128)(2,1)S(1)} %shard_map.114.refs_1_), channel_id=1, source_target_pairs={{0,1},{1,0},{2,3},{3,2},{4,5},{5,4},{6,7},{7,6},{8,9},{9,8},{10,11... | collective-permute-start | bytes 884744 | tf_op jit(solution)/shard_map/ppermute | solution.py:378
  33.0 6.1 %collective-permute-start.3 = (bf16[576,256]{1,0:T(8,128)(2,1)S(1)}, bf16[576,256]{1,0:T(8,128)(2,1)S(1)}, u32[]{:S(2)}, u32[]{:S(2)}) collective-permute-start(bf16[576,256]{1,0:T(8,128)(2,1)S(1)} %collective-permute-done.2.refs_1_), channel_id=1, source_target_pairs={{0,1},{1,0},{2,3},{3,2},{4,5},{5,4},{6,7},{7,6},{8,9},{9,8},{10,11... | collective-permute-start | bytes 884744 | tf_op jit(solution)/shard_map/ppermute | solution.py:378
  33.0 0.7 %copy-start.3 = (s32[4]{0:T(128)S(1)}, s32[4]{0:T(128)}, u32[]{:S(2)}) copy-start(s32[4]{0:T(128)} %refs_0_.1) | copy-start | bytes 52
  33.7 0.7 %copy-start.4 = (s32[12]{0:T(128)S(1)}, s32[12]{0:T(128)}, u32[]{:S(2)}) copy-start(s32[12]{0:T(128)} %refs_1_.1) | copy-start | bytes 148
  34.4 0.7 %copy-start.5 = (s32[12]{0:T(128)S(1)}, s32[12]{0:T(128)}, u32[]{:S(2)}) copy-start(s32[12]{0:T(128)} %refs_2_.1) | copy-start | bytes 148
  38.0 1.1 %copy-start.1 = (bf16[16,256]{1,0:T(8,128)(2,1)S(1)}, bf16[16,256]{1,0:T(8,128)(2,1)}, u32[]{:S(2)}) copy-start(bf16[16,256]{1,0:T(8,128)(2,1)} %refs_4_.5) | copy-start | bytes 24580
  38.0 1.1 %copy-start.2 = (bf16[16,128]{1,0:T(8,128)(2,1)S(1)}, bf16[16,128]{1,0:T(8,128)(2,1)}, u32[]{:S(2)}) copy-start(bf16[16,128]{1,0:T(8,128)(2,1)} %refs_5_.5) | copy-start | bytes 12292
  40.0 9.2 %collective-permute-start.9 = (bf16[512,256]{1,0:T(8,128)(2,1)S(1)}, bf16[512,256]{1,0:T(8,128)(2,1)S(1)}, u32[]{:S(2)}, u32[]{:S(2)}) collective-permute-start(bf16[512,256]{1,0:T(8,128)(2,1)S(1)} %get-tuple-element.23), channel_id=1, source_target_pairs={{0,8},{8,0},{1,9},{9,1},{2,10},{10,2},{3,11},{11,3},{4,12},{12,4},... | collective-permute-start | bytes 786440 | tf_op jit(solution)/shard_map/ppermute | solution.py:378
  41.0 10.6 %collective-permute-start.8 = (bf16[256,256]{1,0:T(8,128)(2,1)S(1)}, bf16[256,256]{1,0:T(8,128)(2,1)S(1)}, u32[]{:S(2)}, u32[]{:S(2)}) collective-permute-start(bf16[256,256]{1,0:T(8,128)(2,1)S(1)} %get-tuple-element.21), channel_id=1, source_target_pairs={{0,8},{8,0},{1,9},{9,1},{2,10},{10,2},{3,11},{11,3},{4,12},{12,4},... | collective-permute-start | bytes 393224 | tf_op jit(solution)/shard_map/ppermute | solution.py:378
